TPU v7x, 32 devices: a whole 2x2x4 slice. The times are simulated.
32 devices in a mesh: au: 8 (over z, core), vert: 4 (over y, x).
Axes of the slice: x: 2, y: 2, z: 4, core: 2. Of those that a mesh axis runs over, the one named last changes fastest.
Arguments:
- vis_value: float32 [128, 128, 2, 128], P('au', 'vert'), may hold values from -6 to 6
- vis_pos: int32 [128, 128, 2, 128], P('au', 'vert'), may hold values from 0 to 1048575, as said below
- counts: int32 [128, 128], P('au', 'vert'), may hold values from 21 to 128, as said below
- kernel: float32 [8, 128], replicated, may hold values from 0.05 to 0.5
Outputs:
- image: float32 [8192, 8192], P(('au', 'vert'))
Inputs may be any that keep to these rules, and one draw needn't show every extreme that they name: Slot k of patch (p, q) holds a visibility exactly when k < counts[p, q]; in every draw some patch has all 128 slots live. vis_pos[p, q, 0, k] lies in [p * 64 * 128, (p + 1) * 64 * 128) and vis_pos[p, q, 1, k] in [q * 64 * 128, (q + 1) * 64 * 128), in every slot.
All inputs are finite; a program needn't handle non-finite values.
Results may differ from a plain program's by a relative error of at most 0.0003.
Values sent between devices are 32-bit elements; how exact they have to be, the bound alone decides.
A program may use at most 192 MiB of HBM per device.

v0:
```python
import math

import jax
import jax.numpy as jnp
from jax import lax
from jax.sharding import PartitionSpec as P

PATCH = 64
PR = 128
PC = 128


highest = lax.Precision.HIGH


def passed_along(value, axis, steps):
    count = lax.axis_size(axis)
    initial, last = (max(0, -steps), min(count, count - steps))
    return lax.ppermute(value, axis, [(source, source + steps) for source in range(initial, last)])


def fourier(length):
    index_list = jnp.arange(length, dtype=jnp.int32)
    angles = (
        2.0
        * math.pi
        / length
        * (index_list[:, None] * index_list[None, :] % length).astype(jnp.float32)
    )
    return jnp.stack([jnp.cos(angles), jnp.sin(angles)])


def twiddle(outer_size, inner_size, length):
    row_index = jnp.arange(outer_size, dtype=jnp.int32)[:, None]
    col_index = jnp.arange(inner_size, dtype=jnp.int32)[None, :]
    angles = 2.0 * math.pi / length * (row_index * col_index % length).astype(jnp.float32)
    return (jnp.cos(angles), jnp.sin(angles))


def complex_table(length):
    cos, sin = fourier(length)
    return jnp.stack([jnp.stack([cos, -sin]), jnp.stack([sin, cos])])


def row_transform(field):
    band_count, outer_size, _, rows, inner_size = field.shape
    length = outer_size * inner_size
    turn_cos, turn_sin = twiddle(outer_size, inner_size, length)
    product = jnp.einsum(
        "scaq,bqcip->sbiap", complex_table(outer_size), field, precision=highest
    )
    rotated = jnp.stack(
        [
            product[0] * turn_cos - product[1] * turn_sin,
            product[0] * turn_sin + product[1] * turn_cos,
        ]
    )
    result = jnp.einsum(
        "scyp,cbiap->sbiya", complex_table(inner_size), rotated, precision=highest
    )
    return result.reshape(2, band_count * rows, length)


def column_transform(received, image_scale):
    length = received.shape[1]
    item_count = received.shape[3]
    inner_size = length // 128
    outer_size = length // inner_size
    turn_cos, turn_sin = twiddle(outer_size, inner_size, length)
    blocked = received.reshape(2, outer_size, inner_size, item_count)
    product = jnp.einsum(
        "scaq,cqpy->sapy", complex_table(outer_size), blocked, precision=highest
    )
    turn_cos = turn_cos[..., None]
    turn_sin = turn_sin[..., None]
    rotated = jnp.stack(
        [
            product[0] * turn_cos - product[1] * turn_sin,
            product[0] * turn_sin + product[1] * turn_cos,
        ]
    )
    last_table = complex_table(inner_size)[0] * image_scale
    image_rows = jnp.einsum("cbp,capy->yba", last_table, rotated, precision=highest)
    return image_rows.reshape(item_count, length)


def joined(array, group):
    count, lead, slots = array.shape
    blocks = array.reshape(count // group, group, lead, slots)
    before = jnp.roll(blocks[:, group - 1], 1, axis=0)
    return jnp.concatenate([before] + [blocks[:, step] for step in range(group)], axis=-1)


def spread(distance, taps):
    weights = jnp.zeros(distance.shape, jnp.float32)
    for tap_step in range(taps.shape[1]):
        weights = jnp.where(distance == tap_step, taps[:, tap_step][:, None], weights)
    return weights


def band_tiles(values, positions, counts, kernel):
    kernel_width, oversample = kernel.shape
    column_count, _, slot_count = values.shape
    width = 128
    group = width // PATCH
    group_count = column_count // group
    live_mask = jnp.arange(slot_count, dtype=jnp.int32)[None, :] < counts[:, None]
    cell_index = positions // oversample
    fine_index = positions - cell_index * oversample
    selector = (
        fine_index[:, :, None, :] == jnp.arange(oversample, dtype=jnp.int32)[:, None]
    ).astype(jnp.float32)
    taps = jnp.einsum("to,naok->natk", kernel, selector, precision=highest)
    taps = joined(taps.reshape(column_count, 2 * kernel_width, slot_count), group)
    cells = joined(cell_index, group)
    scaled = joined(jnp.where(live_mask[:, None], values, 0.0), group)
    extent = PATCH + kernel_width
    row_distance = (
        jnp.arange(extent, dtype=jnp.int32)[None, :, None] - (cells[:, 0] % PATCH)[:, None]
    )
    starts = jnp.arange(group_count, dtype=jnp.int32) * width
    columns = starts[:, None] + jnp.arange(width, dtype=jnp.int32)
    column_distance = columns[:, :, None] - cells[:, 1][:, None]
    row_weights = spread(row_distance, taps[:, :kernel_width])
    column_weights = spread(column_distance, taps[:, kernel_width:])
    scaled_rows = scaled[:, :, None] * row_weights[:, None]
    return jnp.einsum("mcik,mjk->mcij", scaled_rows, column_weights, precision=highest)


def local(vis_value, vis_pos, counts, kernel):
    kernel_width = kernel.shape[0]
    device_count = lax.axis_size("au") * lax.axis_size("vert")
    slot_count = vis_value.shape[3]
    image_scale = 1.0 / math.sqrt(PR * PC * slot_count)
    vert_count = lax.axis_size("vert")
    band_count = vis_value.shape[0] // vert_count
    local_columns = vis_value.shape[1]
    moved_values = lax.all_to_all(
        vis_value.reshape(vert_count, band_count, local_columns, 2, slot_count),
        "vert",
        split_axis=0,
        concat_axis=2,
        tiled=True,
    )
    positions, tallies = (
        lax.all_to_all(
            vis_pos.reshape(vert_count, band_count, local_columns, 2, slot_count),
            "vert",
            split_axis=0,
            concat_axis=2,
            tiled=True,
        ),
        lax.all_to_all(
            counts.reshape(vert_count, band_count, local_columns),
            "vert",
            split_axis=0,
            concat_axis=2,
            tiled=True,
        ),
    )
    column_count = local_columns * vert_count
    values = moved_values.reshape(band_count, column_count, 2, slot_count)
    positions = positions.reshape(band_count, column_count, 2, slot_count)
    tallies = tallies.reshape(band_count, column_count)
    tiles = lax.map(lambda members: band_tiles(*members, kernel), (values, positions, tallies))
    spill = tiles[..., PATCH:, :]
    arrived = passed_along(spill[-1], ("au", "vert"), 1)
    above = jnp.concatenate([arrived[None], spill[:-1]], axis=0)
    field = jnp.concatenate(
        [tiles[..., :kernel_width, :] + above, tiles[..., kernel_width:PATCH, :]], axis=3
    )
    row_field = row_transform(field)
    length = row_field.shape[2]
    column_share = length // device_count
    return column_transform(
        lax.all_to_all(
            row_field.reshape(2, row_field.shape[1], device_count, column_share),
            ("au", "vert"),
            split_axis=2,
            concat_axis=1,
            tiled=True,
        ),
        image_scale,
    )


def solution(mesh):
    in_specs = (P("au", "vert", None, None), P("au", "vert", None, None), P("au", "vert"), P())
    out_specs = P(("au", "vert"), None)
    return jax.shard_map(local, mesh=mesh, in_specs=in_specs, out_specs=out_specs, check_vma=False)
```

profile of v0, /device:TPU:0, one launch (start us, length us, event | category | flops | bytes accessed | tf_op | source)
XLA Modules:
  0.0 779.1 jit_solution(10357679683218870775)
XLA Ops:
  1.4 5.2 all-to-all-start
  6.5 1.9 copy.102
  8.4 2.6 all-to-all-done
  11.1 3.5 all-to-all-start.1
  14.6 1.9 copy.104
  16.5 5.1 all-to-all-done.1
  21.5 3.5 all-to-all-start.2
  28.0 3.6 all-to-all-done.2
  31.6 147.3 %while.12 = (s32[]{:T(128)}, f32[4,64,2,72,128]{4,1,2,3,0:T(8,128)}, s32[4,128]{1,0:T(4,128)S(1)}, f32[4,128,2,128]{3,1,2,0:T(8,128)S(1)}, s32[4,128,2,128]{3,1,2,0:T(8,128)S(1)}, /*index=5*/f32[8,128]{1,0:T(8,128)}, s32[]{:T(128)}) while((s32[]{:T(128)}, f32[4,64,2,72,128]{4,1,2,3,0:T(8,128)}, s32[4,128]{1,0:T(4,128)S(1)}, ...), condition=%wide.region_1.2_spmd, body=%wide.region_0.1_spmd.sunk | while | flops 3013378048 | bytes 48205400 | solution.py:165
  31.8 4.8 fusion.149
  36.9 1.4 fusion.150
  39.0 6.2 select_select_fusion.2
  46.2 18.5 %fusion.155 = f32[1,64,2,72,128]{4,3,2,1,0:T(8,128)S(1)} fusion(f32[64,384]{1,0:T(8,128)S(1)} %get-tuple-element.240, f32[64,384]{1,0:T(8,128)S(1)} %get-tuple-element.241, f32[64,384]{1,0:T(8,128)S(1)} %get-tuple-element.244, f32[64,384]{1,0:T(8,128)S(1)} %get-tuple-element.245, f32[64,384]{1,0:T(8,128)S(1)} %get-tuple-element.248, ...), kind=kOutput, calls=%fused_computation.54.clone.1 | convolution fusion | flops 2774925312 | bytes 12910592 | tf_op jit(solution)/shard_map/while/body/eval_jaxpr/mcik,mjk->mcij/dot_general | solution.py:127
  64.8 3.6 copy_dynamic-update-slice_fusion.2
  68.6 4.8 fusion.149
  73.6 1.4 fusion.150
  75.7 6.2 select_select_fusion.2
  82.9 18.5 %fusion.155 = f32[1,64,2,72,128]{4,3,2,1,0:T(8,128)S(1)} fusion(f32[64,384]{1,0:T(8,128)S(1)} %get-tuple-element.240, f32[64,384]{1,0:T(8,128)S(1)} %get-tuple-element.241, f32[64,384]{1,0:T(8,128)S(1)} %get-tuple-element.244, f32[64,384]{1,0:T(8,128)S(1)} %get-tuple-element.245, f32[64,384]{1,0:T(8,128)S(1)} %get-tuple-element.248, ...), kind=kOutput, calls=%fused_computation.54.clone.1 | convolution fusion | flops 2774925312 | bytes 12910592 | tf_op jit(solution)/shard_map/while/body/eval_jaxpr/mcik,mjk->mcij/dot_general | solution.py:127
  101.5 3.6 copy_dynamic-update-slice_fusion.2
  105.3 4.8 fusion.149
  110.4 1.4 fusion.150
  112.5 6.2 select_select_fusion.2
  119.7 18.5 %fusion.155 = f32[1,64,2,72,128]{4,3,2,1,0:T(8,128)S(1)} fusion(f32[64,384]{1,0:T(8,128)S(1)} %get-tuple-element.240, f32[64,384]{1,0:T(8,128)S(1)} %get-tuple-element.241, f32[64,384]{1,0:T(8,128)S(1)} %get-tuple-element.244, f32[64,384]{1,0:T(8,128)S(1)} %get-tuple-element.245, f32[64,384]{1,0:T(8,128)S(1)} %get-tuple-element.248, ...), kind=kOutput, calls=%fused_computation.54.clone.1 | convolution fusion | flops 2774925312 | bytes 12910592 | tf_op jit(solution)/shard_map/while/body/eval_jaxpr/mcik,mjk->mcij/dot_general | solution.py:127
  138.2 3.7 copy_dynamic-update-slice_fusion.2
  142.1 4.8 fusion.149
  147.2 1.4 fusion.150
  149.3 6.2 select_select_fusion.2
  156.5 18.5 %fusion.155 = f32[1,64,2,72,128]{4,3,2,1,0:T(8,128)S(1)} fusion(f32[64,384]{1,0:T(8,128)S(1)} %get-tuple-element.240, f32[64,384]{1,0:T(8,128)S(1)} %get-tuple-element.241, f32[64,384]{1,0:T(8,128)S(1)} %get-tuple-element.244, f32[64,384]{1,0:T(8,128)S(1)} %get-tuple-element.245, f32[64,384]{1,0:T(8,128)S(1)} %get-tuple-element.248, ...), kind=kOutput, calls=%fused_computation.54.clone.1 | convolution fusion | flops 2774925312 | bytes 12910592 | tf_op jit(solution)/shard_map/while/body/eval_jaxpr/mcik,mjk->mcij/dot_general | solution.py:127
  175.0 3.6 copy_dynamic-update-slice_fusion.2
  180.0 3.4 collective-permute-start
  184.2 1.5 slice.264
  185.7 13.6 %slice.265 = f32[4,64,2,56,128]{4,1,2,3,0:T(8,128)} slice(f32[4,64,2,72,128]{4,1,2,3,0:T(8,128)} %get-tuple-element.85), slice={[0:4], [0:64], [0:2], [8:64], [0:128]} | slice | bytes 29360128 | tf_op jit(solution)/shard_map/slice | solution.py:170
  199.3 2.0 maximum_add_fusion
  201.3 13.5 %fusion.77 = f32[2,4,64,64,128]{4,3,0,2,1:T(8,128)} fusion(f32[4,64,2,56,128]{4,1,2,3,0:T(8,128)} %slice.265, f32[4,64,2,8,128]{4,1,2,3,0:T(8,128)S(1)} %maximum_add_fusion, f32[1,2,64,64]{3,2,1,0:T(8,128)S(1)} %get-tuple-element.147, f32[1,2,64,64]{3,2,1,0:T(8,128)S(1)} %get-tuple-element.146), kind=kOutput, calls=%fused_computation.136 | convolution fusion | flops 3225436160 | bytes 33619968 | tf_op jit(solution)/shard_map/scaq,bqcip->sbiap/dot_general | solution.py:49
  214.8 9.8 %multiply_subtract_fusion.1 = (f32[1,4,64,64,128]{4,3,0,2,1:T(8,128)S(1)}, f32[1,4,64,64,128]{4,3,0,2,1:T(8,128)}) fusion(f32[2,4,64,64,128]{4,3,0,2,1:T(8,128)} %fusion.77, f32[64,128]{1,0:T(8,128)S(1)} %copy-done.2, f32[64,128]{1,0:T(8,128)S(1)} %copy-done.3), kind=kLoop, calls=%fused_computation.140 | loop fusion | flops 12582912 | bytes 33619968 | tf_op jit(solution)/shard_map/sub | solution.py:54
  224.6 12.7 %fusion.76 = f32[2,4,64,128,64]{3,4,0,2,1:T(8,128)} fusion(f32[1,4,64,64,128]{4,3,0,2,1:T(8,128)} %get-tuple-element.143, f32[1,4,64,64,128]{4,3,0,2,1:T(8,128)S(1)} %get-tuple-element.142, f32[1,2,128,128]{3,2,1,0:T(8,128)S(1)} %get-tuple-element.145, f32[1,2,128,128]{3,2,1,0:T(8,128)S(1)} %get-tuple-element.144), kind=kOutput, calls=%fused_computation.135 | convolution fusion | flops 6446710784 | bytes 33816576 | tf_op jit(solution)/shard_map/scyp,cbiap->sbiya/dot_general | solution.py:58
  237.2 23.0 %copy.110 = f32[2,4,64,128,64]{4,3,2,1,0:T(8,128)} copy(f32[2,4,64,128,64]{3,4,0,2,1:T(8,128)} %fusion.76) | data formatting | bytes 33554432 | tf_op jit(solution)/shard_map/scyp,cbiap->sbiya/transpose | solution.py:58
  260.3 27.9 %reshape_reshape.3 = f32[2,256,32,256]{3,2,1,0:T(8,128)} reshape(f32[2,4,64,128,64]{4,3,2,1,0:T(8,128)} %copy.110) | data formatting | bytes 33554432 | tf_op jit(solution)/shard_map/reshape;reshape | solution.py:177
  288.2 15.9 %copy.111 = f32[2,256,32,256]{3,1,0,2:T(8,128)} copy(f32[2,256,32,256]{3,2,1,0:T(8,128)} %reshape_reshape.3) | data formatting | bytes 33554432 | tf_op jit(solution)/shard_map/reshape;reshape | solution.py:177
  304.1 5.2 all-to-all-start.3
  309.4 382.5 %all-to-all-done.3 = f32[2,256,32,256]{3,1,0,2:T(8,128)} async-done(((f32[2,256,32,256]{3,1,0,2:T(8,128)}), f32[2,256,32,256]{3,1,0,2:T(8,128)}, u32[]{:S(2)}, u32[]{:S(2)}) %all-to-all-start.3) | async-done | bytes 16777248 | tf_op jit(solution)/shard_map/all_to_all | solution.py:176
  691.9 11.5 %copy.112 = f32[2,256,32,256]{3,1,2,0:T(8,128)} copy(f32[2,256,32,256]{3,1,0,2:T(8,128)} %all-to-all-done.3) | data formatting | bytes 33554432 | tf_op jit(solution)/shard_map/all_to_all | solution.py:176
  703.4 25.9 %fusion.78 = f32[2,128,64,256]{3,1,2,0:T(8,128)} fusion(f32[2,128,64,256]{3,2,1,0:T(8,128)} %bitcast.254, f32[1,2,128,128]{3,2,1,0:T(8,128)S(1)} %get-tuple-element.145, f32[1,2,128,128]{3,2,1,0:T(8,128)S(1)} %get-tuple-element.144), kind=kOutput, calls=%fused_computation.141 | convolution fusion | flops 6442516480 | bytes 33816576 | tf_op jit(solution)/shard_map/scaq,cqpy->sapy/dot_general | solution.py:71
  729.3 9.8 %multiply_subtract_fusion = (f32[1,128,64,256]{3,1,2,0:T(8,128)S(1)}, f32[1,128,64,256]{3,1,2,0:T(8,128)}) fusion(f32[2,128,64,256]{3,1,2,0:T(8,128)} %fusion.78, f32[128,64]{0,1:T(8,128)S(1)} %get-tuple-element.154, f32[128,64]{0,1:T(8,128)S(1)} %get-tuple-element.155), kind=kLoop, calls=%fused_computation.138 | loop fusion | flops 12582912 | bytes 33619968 | tf_op jit(solution)/shard_map/sub | solution.py:78
  739.1 4.6 pad_maximum_fusion.2
  743.8 14.5 %fusion.81 = f32[256,64,128]{0,1,2:T(8,128)} fusion(f32[2,128,64,256]{3,1,2,0:T(8,128)S(1)} %pad_maximum_fusion.2, f32[1,64,64]{2,1,0:T(8,128)S(1)} %fusion.125, f32[1,64,64]{2,1,0:T(8,128)S(1)} %copy-done), kind=kOutput, calls=%fused_computation.142 | convolution fusion | flops 1610629120 | bytes 25198592 | tf_op jit(solution)/shard_map/cbp,capy->yba/dot_general | solution.py:83
  758.3 11.5 %copy.115 = f32[256,64,128]{0,2,1:T(8,128)} copy(f32[256,64,128]{0,1,2:T(8,128)} %fusion.81) | data formatting | bytes 16777216 | tf_op jit(solution)/shard_map/cbp,capy->yba/transpose | solution.py:83
  769.8 8.9 %copy.116 = f32[256,8192]{1,0:T(8,128)} copy(f32[256,8192]{0,1:T(8,128)} %bitcast.258) | data formatting | bytes 16777216 | tf_op jit(solution)/shard_map/reshape | solution.py:84
  (163 shorter events, 13.9 us)
Async XLA Ops:
  1.4 9.7 %all-to-all-start = ((s32[4,1,128]{2,1,0:T(1,128)}), s32[4,1,128]{2,1,0:T(1,128)S(1)}, u32[]{:S(2)}, u32[]{:S(2)}) async-start(s32[4,1,128]{2,1,0:T(1,128)} %reshape.440), calls=%async_computation | async-start | bytes 4096 | tf_op jit(solution)/shard_map/all_to_all | solution.py:153
  11.1 10.5 %all-to-all-start.1 = ((f32[4,4,32,2,128]{4,2,3,1,0:T(8,128)}), f32[4,4,32,2,128]{4,2,3,1,0:T(8,128)S(1)}, u32[]{:S(2)}, u32[]{:S(2)}) async-start(f32[4,4,32,2,128]{4,2,3,1,0:T(8,128)} %bitcast.32), calls=%async_computation.1 | async-start | bytes 1048576 | tf_op jit(solution)/shard_map/all_to_all | solution.py:138
  21.5 10.0 %all-to-all-start.2 = ((s32[4,4,32,2,128]{4,2,3,1,0:T(8,128)}), s32[4,4,32,2,128]{4,2,3,1,0:T(8,128)S(1)}, u32[]{:S(2)}, u32[]{:S(2)}) async-start(s32[4,4,32,2,128]{4,2,3,1,0:T(8,128)} %bitcast.36), calls=%async_computation.2 | async-start | bytes 1048576 | tf_op jit(solution)/shard_map/all_to_all | solution.py:146
  31.6 152.5 %copy-start = (f32[1,64,64]{2,1,0:T(8,128)S(1)}, f32[1,64,64]{2,1,0:T(8,128)}, u32[]{:S(2)}) copy-start(f32[1,64,64]{2,1,0:T(8,128)} %get-tuple-element.149) | copy-start | bytes 49156
  31.6 152.5 %copy-start.1 = (f32[1,64,64]{2,1,0:T(8,128)S(1)}, f32[1,64,64]{2,1,0:T(8,128)}, u32[]{:S(2)}) copy-start(f32[1,64,64]{2,1,0:T(8,128)} %get-tuple-element.148) | copy-start | bytes 49156
  180.0 19.3 %collective-permute-start = (f32[64,2,8,128]{3,0,1,2:T(8,128)S(1)}, f32[64,2,8,128]{3,0,1,2:T(8,128)S(1)}, u32[]{:S(2)}, u32[]{:S(2)}) collective-permute-start(f32[64,2,8,128]{3,0,1,2:T(8,128)S(1)} %slice_bitcast_fusion.7), channel_id=1, source_target_pairs={{0,1},{1,2},{2,3},{3,4},{4,5},{5,6},{6,7},{7,8},{8,9},{9,10},{10,1... | collective-permute-start | bytes 1572872 | tf_op jit(solution)/shard_map/ppermute | solution.py:19
  201.3 13.5 %copy-start.2 = (f32[64,128]{1,0:T(8,128)S(1)}, f32[64,128]{1,0:T(8,128)}, u32[]{:S(2)}) copy-start(f32[64,128]{1,0:T(8,128)} %get-tuple-element.150) | copy-start | bytes 98308
  201.3 13.5 %copy-start.3 = (f32[64,128]{1,0:T(8,128)S(1)}, f32[64,128]{1,0:T(8,128)}, u32[]{:S(2)}) copy-start(f32[64,128]{1,0:T(8,128)} %get-tuple-element.151) | copy-start | bytes 98308
  304.1 387.9 %all-to-all-start.3 = ((f32[2,256,32,256]{3,1,0,2:T(8,128)}), f32[2,256,32,256]{3,1,0,2:T(8,128)}, u32[]{:S(2)}, u32[]{:S(2)}) async-start(f32[2,256,32,256]{3,1,0,2:T(8,128)} %copy.111), calls=%async_computation.3 | async-start | bytes 33554432 | tf_op jit(solution)/shard_map/all_to_all | solution.py:176
where the time goes:
time: 791 us; the launch traced here: 779 us
  waiting for transfers between devices  394 us (50%)
  matrix products  160 us (20%)
  local copies, waits for them, and re-layouts  145 us (18%)
  other arithmetic  57.6 us (7%)
  starting transfers between devices  20.7 us (3%)
    all_to_all x1, waiting for transfers between devices, local(): lax.all_to_all(row_field.reshape(2, row_field.shape[1], device_count, col...  383 us
    dot_general x4, matrix products, band_tiles(): jnp.einsum('mcik,mjk->mcij', scaled_rows, column_weights, precision=highest)  74.2 us
    another operation x2, local copies, waits for them, and re-layouts, local(): row_field.reshape(2, row_field.shape[1], device_count, column_share)  43.8 us
    dot_general x1, matrix products, column_transform(): jnp.einsum('scaq,cqpy->sapy', complex_table(outer_size), blocked, precisi...  25.9 us
    select_n x4, other arithmetic, spread(): jnp.where(distance == tap_step, taps[:, tap_step][:, None], weights)  24.8 us
    transpose x1, local copies, waits for them, and re-layouts, row_transform(): jnp.einsum('scyp,cbiap->sbiya', complex_table(inner_size), rotated, preci...  23 us
    dot_general x4, matrix products, band_tiles(): taps = jnp.einsum('to,naok->natk', kernel, selector, precision=highest)  19.3 us
  transfers between devices with their start and end apart: 5, of which 4 were waited for; matrix products, arithmetic and copies ran while one was open for 3% of the time, Pallas kernels for 0%

commit v1 on v0

v1 whole, which is shorter than its diff:
```python
import functools
import math

import jax
import jax.numpy as jnp
from jax import lax
from jax.experimental import pallas as pl
from jax.experimental.pallas import tpu as pltpu
from jax.sharding import Mesh, PartitionSpec as P

PATCH = 64
LANES = 128
SUB = 8

BF16 = jnp.bfloat16
F32 = jnp.float32


def split(x):
    hi = x.astype(BF16)
    lo = (x - hi.astype(F32)).astype(BF16)
    return hi, lo


def dot(lhs, rhs):
    return lax.dot_general(lhs, rhs, (((1,), (0,)), ((), ())), preferred_element_type=F32)


def dot_nt(lhs, rhs):
    return lax.dot_general(lhs, rhs, (((1,), (1,)), ((), ())), preferred_element_type=F32)


def turn(product, length):
    angle = (2.0 * math.pi / length) * (product % length).astype(F32)
    return jnp.cos(angle), jnp.sin(angle)


def real_parts(cos, sin):
    return jnp.stack([jnp.stack([cos, -sin]), jnp.stack([sin, cos])])


def tap_blocks(kern, cells, base, mirrored, length, wrap):
    slots = cells.shape[1]
    shape = (SUB, slots)
    cell = lax.shift_right_logical(cells, 7)
    fine = jnp.broadcast_to(cells & 127, shape)
    taps = jnp.take_along_axis(kern, fine, axis=1, mode="promise_in_bounds")
    sub = lax.broadcasted_iota(jnp.int32, shape, 0)
    taps = jnp.where(jnp.broadcast_to(cell, shape) + sub < length, taps, 0.0)
    off = jnp.broadcast_to(cell & (PATCH - 1), shape)
    if mirrored:
        place = base + PATCH - off
        tap = (place - sub) & (SUB - 1)
        block = lax.shift_right_arithmetic(place - tap, 3)
    else:
        place = base + off
        tap = (sub - place) & (SUB - 1)
        block = lax.shift_right_arithmetic(place + tap, 3)
    if wrap:
        block = block & (wrap - 1)
    turned = jnp.take_along_axis(taps, tap, axis=0, mode="promise_in_bounds")
    return turned, block


def patch_operands(kern, fields, mirrored, parity, length):
    values_re, values_im = fields[0:1], fields[1:2]
    cells = fields[2:4].astype(jnp.int32)
    rows, row_block = tap_blocks(kern, cells[0:1], SUB, mirrored, length, 0)
    cols, col_block = tap_blocks(kern, cells[1:2], PATCH * parity, mirrored, length, 2 * PATCH // SUB)
    if mirrored:
        values_im = -values_im

    def halves(x):
        hi = x.astype(BF16).astype(F32)
        return hi, x - hi

    row_hi, row_lo = halves(rows)
    row_masks = [row_block == j for j in range(PATCH // SUB + 2)]
    a_hi = jnp.concatenate([jnp.where(m, row_hi, 0.0) for m in row_masks], axis=0).astype(BF16)
    a_lo = jnp.concatenate([jnp.where(m, row_lo, 0.0) for m in row_masks], axis=0).astype(BF16)
    col_masks = [col_block == j for j in range(2 * PATCH // SUB)]
    live = [(j - parity * (PATCH // SUB)) % len(col_masks) in (*range(9), 15) for j in range(len(col_masks))]
    zero = jnp.zeros_like(cols)
    b_hi, b_lo = [], []
    for value in (values_re, values_im):
        hi, lo = halves(cols * value)
        b_hi += [jnp.where(m, hi, 0.0) if on else zero for m, on in zip(col_masks, live)]
        b_lo += [jnp.where(m, lo, 0.0) if on else zero for m, on in zip(col_masks, live)]
    return a_hi, a_lo, jnp.concatenate(b_hi, axis=0).astype(BF16), jnp.concatenate(b_lo, axis=0).astype(BF16)


def tile_of(kern, low, high, parity, length):
    la_hi, la_lo, lb_hi, lb_lo = patch_operands(kern, low, False, parity, length)
    ha_hi, ha_lo, hb_hi, hb_lo = patch_operands(kern, high, True, parity, length)
    a_hi = jnp.concatenate([la_hi, ha_hi], axis=1)
    a_lo = jnp.concatenate([la_lo, ha_lo], axis=1)
    b_hi = jnp.concatenate([lb_hi, hb_hi], axis=1)
    b_lo = jnp.concatenate([lb_lo, hb_lo], axis=1)
    rows = a_hi.shape[0]
    main = dot_nt(jnp.concatenate([a_hi, a_lo], axis=0), b_hi)
    return main[:rows] + main[rows:] + dot_nt(a_hi, b_lo)


def grid_kernel(dims, flags_ref, own_ref, par_ref, kern_ref, f1_ref, tw_ref, eh_ref, el_ref, h_ref, g_ref, carry_ref):
    bands, pairs, row_stride, length = dims
    tile_rows = PATCH + 2 * SUB
    is_low = flags_ref[0] == 1
    is_last = flags_ref[1] == 1
    kern = kern_ref[...]
    parts = 2 * pairs
    lane = lax.broadcasted_iota(jnp.int32, (tile_rows, 2 * LANES), 1) & (LANES - 1)

    def clear(n, _):
        for part in range(2):
            base = pl.multiple_of((part * pairs + n) * row_stride, SUB)
            g_ref[pl.ds(base, row_stride), :] = jnp.zeros((row_stride, LANES), F32)
        return 0

    lax.fori_loop(0, pairs, clear, 0)

    for band in range(bands):

        def fields_at(q, parity):
            own_low = own_ref[band, q, 4 * parity : 4 * parity + 4, :]
            par_low = par_ref[band, q, 4 * parity : 4 * parity + 4, :]
            mq = pairs - 1 - q
            mp = 1 - parity
            own_high = own_ref[bands - 1 - band, mq, 4 * mp : 4 * mp + 4, :]
            par_high = par_ref[bands - 1 - band, mq, 4 * mp : 4 * mp + 4, :]
            return jnp.where(is_low, own_low, par_low), jnp.where(is_low, par_high, own_high)

        def columns(q):
            odd = tile_of(kern, *fields_at(q, 1), 1, length)
            nxt = jnp.where(q == pairs - 1, 0, q + 1)
            even = tile_of(kern, *fields_at(nxt, 0), 0, length)
            here = jnp.where(lane < SUB, 0.0, odd) + jnp.where(lane < LANES - SUB, 0.0, even)
            there = jnp.where(lane < SUB, odd, 0.0) + jnp.where(lane < LANES - SUB, even, 0.0)
            return here, there

        _, there = columns(pairs - 1)
        carry_ref[...] = there

        def step(q, _):
            here, there = columns(q)
            total = here + carry_ref[...]
            carry_ref[...] = there
            for part in range(2):
                base = pl.multiple_of((part * pairs + q) * row_stride, SUB) + band * PATCH
                where = pl.ds(base, tile_rows)
                g_ref[where, :] = g_ref[where, :] + total[:, part * LANES : (part + 1) * LANES]
            return 0

        lax.fori_loop(0, pairs, step, 0)

        cos = tw_ref[0]
        sin = tw_ref[1]

        def quad(group, _):
            first = band * PATCH + 4 * group
            lines = []
            for pair in range(2):
                cells = []
                for one in range(2):
                    row = first + 2 * pair + one
                    up = bands * PATCH + SUB
                    j = row - up
                    moved = jnp.where(j == 6, 0, jnp.where(j == 7, 7, jnp.where(j % 2 == 0, j + 2, j)))
                    row = jnp.where(is_last & (j >= 0), up + moved, row)
                    cells.append(g_ref[pl.ds(row, parts, stride=row_stride), :])
                hi, lo = split(jnp.concatenate(cells, axis=1))
                out = dot(f1_ref[...], jnp.concatenate([hi, lo], axis=0))
                out = out[:parts] + out[parts:]
                for one in range(2):
                    re = out[:pairs, one * LANES : (one + 1) * LANES]
                    im = out[pairs:, one * LANES : (one + 1) * LANES]
                    lines.append(jnp.concatenate([re * cos - im * sin, re * sin + im * cos], axis=1))
            hi, lo = split(jnp.concatenate(lines, axis=0))
            count = el_ref.shape[0]
            out = dot_nt(eh_ref[...], hi)
            out = out[:count] + out[count:] + dot_nt(el_ref[...], lo)
            dests, _, share, _ = h_ref.shape
            for part in range(2):
                piece = out[:, part * LANES : (part + 1) * LANES].reshape(dests, share, LANES)
                h_ref[:, first // 2 + part, :, :] = piece
            return 0

        groups = PATCH // 4 + (2 * SUB // 4 if band == bands - 1 else 0)
        lax.fori_loop(0, groups, quad, 0)


def grid_and_rows(flags, own, par, kern, f1, tw, eh, el, dests, length):
    bands, pairs = own.shape[0], own.shape[1]
    rows = bands * PATCH + 2 * SUB
    row_stride = rows + SUB
    outs = el.shape[0]
    vmem = pl.BlockSpec(memory_space=pltpu.VMEM)
    return pl.pallas_call(
        functools.partial(grid_kernel, (bands, pairs, row_stride, length)),
        out_shape=jax.ShapeDtypeStruct((dests, rows * pairs // LANES, outs // dests, LANES), F32),
        in_specs=[pl.BlockSpec(memory_space=pltpu.SMEM)] + [vmem] * 7,
        out_specs=vmem,
        scratch_shapes=[
            pltpu.VMEM((2 * pairs * row_stride, LANES), F32),
            pltpu.VMEM((PATCH + 2 * SUB, 2 * LANES), F32),
        ],
        compiler_params=pltpu.CompilerParams(vmem_limit_bytes=60 * 1024 * 1024),
        name="grid_rows",
    )(flags, own, par, kern, f1, tw, eh, el)


def column_kernel(dims, flags_ref, h_ref, f2_ref, f2l_ref, tw_ref, e2_ref, out_ref, r_ref, z_ref, s_ref, sems):
    sources, spans, bands, block_rows = dims
    share = 2 * spans
    low = flags_ref[0] == 1
    width = LANES
    y_count = spans * PATCH
    half = PATCH // 2

    blocks = h_ref.shape[1]
    stride = (blocks + 1) * share

    @pl.when(pl.program_id(0) == 0)
    def _():
        copies = [
            pltpu.make_async_copy(h_ref.at[n], r_ref.at[pl.ds(n * (blocks + 1), blocks)], sems.at[n])
            for n in range(sources)
        ]
        for copy in copies:
            copy.start()
        for copy in copies:
            copy.wait()
        flat = r_ref.reshape(sources * stride, width)
        up_block = SUB // 2 + bands * half
        sub = lax.broadcasted_iota(jnp.int32, (share, width), 0)
        sign = jnp.where(sub % 2 == 0, 1.0, -1.0)

        def at_block(n, block):
            source = jnp.where(low, n, sources - 1 - n)
            return source * (blocks + 1) + block

        def add(to, value):
            r_ref[to] = r_ref[to] + value

        def neighbours(n, _):
            for t in range(SUB // 2):
                add(at_block(n + 1, SUB // 2 + t), r_ref[at_block(n, up_block + t)])
                add(at_block(n, up_block - SUB // 2 + t), r_ref[at_block(n + 1, t)])
            return 0

        lax.fori_loop(0, sources - 1, neighbours, 0)
        for t in range(SUB // 2 - 1):
            add(at_block(sources - 1, up_block - 1 - t), sign * r_ref[at_block(sources - 1, up_block + t)])
        top = r_ref[at_block(sources - 1, up_block + SUB // 2 - 1)]
        lane = lax.broadcasted_iota(jnp.int32, (share, width), 1)
        lifted = jnp.concatenate([top[share - 1 :], top[: share - 1]], axis=0)
        first = at_block(0, SUB // 2)
        r_ref[first] = jnp.where((sub % 2 == 1) & (lane < PATCH), lifted, r_ref[first])

        odd = lax.broadcasted_iota(jnp.int32, (PATCH, width), 1) % 2
        flip = jnp.where(odd == 0, 1.0, -1.0)

        def pair_step(rho, _):
            tall = []
            for k in range(spans):
                cells = []
                for c in range(2):
                    for i in range(bands):
                        row = (SUB // 2 + i * half + rho) * share + 2 * k + c
                        cells.append(flat[pl.ds(row, sources, stride=stride), :])
                tall.append(jnp.concatenate(cells, axis=0).T)
            x = jnp.concatenate(tall, axis=0)
            hi, lo = split(x)
            z = dot(jnp.concatenate([hi, lo], axis=1), f2_ref[...]) + dot(hi, f2l_ref[...])
            top_col = jnp.where(low, x[:, PATCH : PATCH + 1], x[:, PATCH + sources - 1 : PATCH + sources])
            for k in range(spans):
                for one in range(2):
                    at = (2 * k + one) * PATCH
                    re = z[at : at + PATCH, :width]
                    im = z[at : at + PATCH, width:]
                    line = 2 * rho + one
                    cos = tw_ref[0, pl.ds(line, 1), :]
                    sin = tw_ref[1, pl.ds(line, 1), :]
                    new_re = re * cos - im * sin
                    new_im = re * sin + im * cos
                    if one == 0:
                        nyquist = flip * top_col[at : at + PATCH]
                        new_im = jnp.where(rho == 0, nyquist, new_im)
                    z_ref[pl.ds(pl.multiple_of(line * y_count + k * PATCH, PATCH), PATCH), :] = new_re
                    z_ref[pl.ds(pl.multiple_of((PATCH + line) * y_count + k * PATCH, PATCH), PATCH), :] = new_im
            return 0

        lax.fori_loop(0, half, pair_step, 0)

    start = pl.program_id(0) * block_rows

    def eight(group, _):
        for pair in range(SUB // 2):
            y = start + group * SUB + 2 * pair
            cells = [z_ref[pl.ds(y + one, 2 * PATCH, stride=y_count), :] for one in range(2)]
            hi, lo = split(jnp.concatenate(cells, axis=1))
            out = dot(e2_ref[...], jnp.concatenate([hi, lo], axis=0))
            out = out[:PATCH] + out[PATCH:]
            for one in range(2):
                s_ref[pl.ds(2 * pair + one, PATCH, stride=SUB), :] = out[:, one * width : (one + 1) * width]
        at = pl.ds(pl.multiple_of(group * SUB, SUB), SUB)
        for block in range(PATCH):
            out_ref[at, block * width : (block + 1) * width] = s_ref[block * SUB : (block + 1) * SUB, :]
        return 0

    lax.fori_loop(0, block_rows // SUB, eight, 0)


def columns_of(flags, h, f2, f2l, tw, e2, sources, spans, bands, length):
    y_count = spans * PATCH
    block_rows = min(32, y_count)
    vmem = pl.BlockSpec(memory_space=pltpu.VMEM)
    return pl.pallas_call(
        functools.partial(column_kernel, (sources, spans, bands, block_rows)),
        grid=(y_count // block_rows,),
        out_shape=jax.ShapeDtypeStruct((y_count, length), F32),
        in_specs=[pl.BlockSpec(memory_space=pltpu.SMEM), pl.BlockSpec(memory_space=pl.ANY)] + [vmem] * 4,
        out_specs=pl.BlockSpec((block_rows, length), lambda n: (n, 0)),
        scratch_shapes=[
            pltpu.VMEM((sources * (h.shape[1] + 1), h.shape[2], LANES), F32),
            pltpu.VMEM((2 * PATCH * y_count, LANES), F32),
            pltpu.VMEM((PATCH * SUB, LANES), F32),
            pltpu.SemaphoreType.DMA((sources,)),
        ],
        compiler_params=pltpu.CompilerParams(vmem_limit_bytes=60 * 1024 * 1024),
        name="columns",
    )(flags, h, f2, f2l, tw, e2)


def split_table(x):
    rounded = lax.reduce_precision(x, 8, 7)
    return rounded.astype(BF16), (x - rounded).astype(BF16)


def stacked(table):
    hi, lo = split_table(table)
    return jnp.concatenate([jnp.concatenate([hi, hi], axis=1), jnp.concatenate([lo, jnp.zeros_like(lo)], axis=1)], axis=0)


def local(vis_value, vis_pos, counts, kernel, *, au, vert):
    devices = au * vert
    half_au = au // 2
    axes = ("half", "sub", "vert")
    me = lax.axis_index(axes)
    low = me < devices // 2
    slots = vis_value.shape[3]
    bands = vis_value.shape[0] // vert
    local_cols = vis_value.shape[1]
    cols = local_cols * vert
    pairs = cols // 2
    length = cols * PATCH
    rows_of_patches = vis_value.shape[0] * au
    scale = 1.0 / math.sqrt(rows_of_patches * cols * slots)
    sources = devices // 2
    y_count = length // devices
    spans = y_count // PATCH

    live = jnp.arange(slots, dtype=jnp.int32) < counts[:, :, None, None]
    fields = jnp.concatenate([jnp.where(live, vis_value, 0.0), vis_pos.astype(F32)], axis=2)
    fields = fields.reshape(vert, bands, local_cols // 2, 8, slots)
    own = lax.all_to_all(fields, "vert", split_axis=0, concat_axis=2, tiled=True)
    own = own.reshape(bands, pairs, 8, slots)
    par = lax.ppermute(own, axes, [(d, devices - 1 - d) for d in range(devices)])

    band_index = jnp.where(low, me, devices - 1 - me)
    flags = jnp.stack([low, band_index == sources - 1]).astype(jnp.int32)

    ya = jnp.arange(pairs, dtype=jnp.int32)
    p = jnp.arange(LANES, dtype=jnp.int32)
    first = real_parts(*turn(ya[:, None] * ya[None, :], pairs))
    f1 = stacked(first.transpose(0, 2, 1, 3).reshape(2 * pairs, 2 * pairs))
    tw1 = jnp.stack(turn(ya[:, None] * p[None, :], length))
    yb = jnp.where(low, 0, LANES // 2) + jnp.arange(LANES // 2, dtype=jnp.int32)
    second = real_parts(*turn(yb[:, None] * p[None, :], LANES))
    second = second.transpose(2, 0, 1, 3).reshape(LANES, 2 * LANES)
    hi, lo = split_table(second)
    h = grid_and_rows(flags, own, par, kernel, f1, tw1, jnp.concatenate([hi, lo], axis=0), hi, sources, length)
    h = lax.all_to_all(h, ("sub", "vert"), split_axis=0, concat_axis=0, tiled=True)

    order = jnp.arange(sources, dtype=jnp.int32)
    order = jnp.where(low, order, sources - 1 - order)
    d = (bands * order[None, :] + jnp.arange(bands, dtype=jnp.int32)[:, None]).reshape(-1)
    xa = jnp.arange(LANES, dtype=jnp.int32)
    table = real_parts(*turn(xa[:, None] * d[None, :], LANES))
    hi, lo = split_table(table.transpose(1, 3, 0, 2).reshape(2 * PATCH, 2 * LANES))
    r = jnp.arange(PATCH, dtype=jnp.int32)
    tw2 = jnp.stack(turn(r[:, None] * xa[None, :], length))
    cos, sin = turn(r[:, None] * r[None, :], PATCH)
    last = jnp.concatenate([cos, jnp.where(r[None, :] == 0, 1.0, -sin)], axis=1) * scale
    return columns_of(
        flags, h, jnp.concatenate([hi, hi], axis=0), lo, tw2, stacked(last), sources, spans, bands, length
    )


def solution(mesh):
    au, vert = mesh.shape["au"], mesh.shape["vert"]
    halves = Mesh(mesh.devices.reshape(2, au // 2, vert), ("half", "sub", "vert"))
    rows = ("half", "sub")
    in_specs = (P(rows, "vert", None, None), P(rows, "vert", None, None), P(rows, "vert"), P())
    return jax.shard_map(
        functools.partial(local, au=au, vert=vert),
        mesh=halves,
        in_specs=in_specs,
        out_specs=P((*rows, "vert"), None),
        check_vma=False,
    )
```

time: 791 us -> 368 us (0.47); the launches traced: 779 us -> 364 us
  waiting for transfers between devices: 394 us -> 140 us
  Pallas kernels: 0 us -> 179 us
  matrix products: 160 us -> 0 us
  local copies, waits for them, and re-layouts: 145 us -> 1.48 us
  other arithmetic: 57.6 us -> 10.8 us
  starting transfers between devices: 20.7 us -> 32.5 us
    all_to_all x4 -> x2, waiting for transfers between devices: 394 us -> 117 us  [the longest x1 104 us: local(): lax.all_to_all(h, ('sub', 'vert'), split_axis=0, concat_axis=0, tiled=True)]
    pallas_call x0 -> x2, Pallas kernels: none -> 179 us  [the longest x1 146 us: grid_and_rows(): pl.pallas_call(functools.partial(grid_kernel, (bands, pairs, row_stride,...]
    dot_general x12 -> x0, matrix products: 160 us -> none  [the longest x4 74.2 us: band_tiles(): jnp.einsum('mcik,mjk->mcij', scaled_rows, column_weights, precision=highest)]
    another operation x2 -> x0, local copies, waits for them, and re-layouts: 43.8 us -> none  [local(): row_field.reshape(2, row_field.shape[1], device_count, column_share)]
    transpose x2, local copies, waits for them, and re-layouts: 34.6 us -> 0.21 us  [the longest x1 0.1 us: local(): second = second.transpose(2, 0, 1, 3).reshape(LANES, 2 * LANES)]
    select_n x12 -> x2, other arithmetic: 26.4 us -> 1.56 us  [the longest x1 1.41 us: local(): jnp.where(live, vis_value, 0.0)]
    ppermute x1, waiting for transfers between devices: 0.01 us -> 22.5 us  [local(): lax.ppermute(own, axes, [(d, devices - 1 - d) for d in range(devices)])]
    slice x38 -> x0, local copies, waits for them, and re-layouts: 22.2 us -> none  [the longest x1 13.6 us: local(): tiles[..., kernel_width:PATCH, :]]
  transfers between devices with their start and end apart: 5 -> 3, of which waited for: 4 -> 3; matrix products, arithmetic and copies ran while one was open for 3% -> 2% of each run, Pallas kernels for 0% -> 0%
where the time goes in v1:
time: 368 us; the launch traced here: 364 us
  Pallas kernels  179 us (49%)
  waiting for transfers between devices  140 us (38%)
  starting transfers between devices  32.5 us (9%)
  other arithmetic  10.8 us (3%)
    pallas_call x1, Pallas kernels, grid_and_rows(): pl.pallas_call(functools.partial(grid_kernel, (bands, pairs, row_stride,...  146 us
    all_to_all x1, waiting for transfers between devices, local(): lax.all_to_all(h, ('sub', 'vert'), split_axis=0, concat_axis=0, tiled=True)  104 us
    pallas_call x1, Pallas kernels, columns_of(): pl.pallas_call(functools.partial(column_kernel, (sources, spans, bands, b...  33.5 us
    all_to_all x1, starting transfers between devices, local(): lax.all_to_all(h, ('sub', 'vert'), split_axis=0, concat_axis=0, tiled=True)  24.3 us
    ppermute x1, waiting for transfers between devices, local(): lax.ppermute(own, axes, [(d, devices - 1 - d) for d in range(devices)])  22.5 us
    all_to_all x1, waiting for transfers between devices, local(): lax.all_to_all(fields, 'vert', split_axis=0, concat_axis=2, tiled=True)  13 us
  transfers between devices with their start and end apart: 3, of which 3 were waited for; matrix products, arithmetic and copies ran while one was open for 2% of the time, Pallas kernels for 0%

profile of v1, /device:TPU:0, one launch (start us, length us, event | category | flops | bytes accessed | tf_op | source)
XLA Modules:
  0.0 364.1 jit_solution(12766666646453118652)
XLA Ops:
  0.0 0.8 iota_compare_fusion.1
  0.8 1.3 convert_element_type.113
  2.1 1.4 broadcast_select_fusion
  3.5 1.5 pad_maximum_fusion
  5.0 5.2 %all-to-all-start = ((f32[4,4,16,8,128]{4,3,2,1,0:T(8,128)}), f32[4,4,16,8,128]{4,3,2,1,0:T(8,128)S(1)}, u32[]{:S(2)}, u32[]{:S(2)}) async-start(f32[4,4,16,8,128]{4,3,2,1,0:T(8,128)} %bitcast.2), calls=%async_computation | async-start | bytes 2097152 | tf_op jit(solution)/shard_map/all_to_all | solution.py:365
  10.2 0.1 fusion.47
  10.3 0.1 fusion.45
  10.5 0.2 fusion.48
  10.8 13.0 %all-to-all-done = f32[4,4,16,8,128]{4,3,2,1,0:T(8,128)S(1)} async-done(((f32[4,4,16,8,128]{4,3,2,1,0:T(8,128)}), f32[4,4,16,8,128]{4,3,2,1,0:T(8,128)S(1)}, u32[]{:S(2)}, u32[]{:S(2)}) %all-to-all-start) | async-done | bytes 1048608 | tf_op jit(solution)/shard_map/all_to_all | solution.py:365
  23.8 0.1 copy.13
  23.9 0.0 copy-start
  23.9 3.0 collective-permute-start
  26.9 0.1 copy.15
  27.0 0.1 copy.14
  27.2 0.1 reshape.452
  27.3 0.6 add_convert_fusion.flags_ref
  27.9 0.1 fusion.41
  28.1 0.6 pad_maximum_fusion.4.tw_ref
  28.7 0.0 copy-start.2
  28.7 0.7 pad_maximum_fusion.1.eh_ref
  29.4 0.7 fusion.3.f1_ref
  30.1 22.5 %collective-permute-done.par_ref = f32[4,64,8,128]{3,2,1,0:T(8,128)S(1)} collective-permute-done((f32[4,64,8,128]{3,2,1,0:T(8,128)S(1)}, f32[4,64,8,128]{3,2,1,0:T(8,128)S(1)}, u32[]{:S(2)}, u32[]{:S(2)}) %collective-permute-start) | collective-permute-done | bytes 1048608 | tf_op jit(solution)/shard_map/ppermute | solution.py:367
  52.6 0.0 copy-done
  52.6 0.0 copy-done.2
  52.6 0.0 copy-start.1
  52.6 1.0 copy-done.1
  53.6 145.7 %grid_rows.1 = f32[16,136,8,128]{3,2,1,0:T(8,128)} custom-call(s32[2]{0:T(128)} %add_convert_fusion.flags_ref, f32[4,64,8,128]{3,2,1,0:T(8,128)} %bitcast.36, f32[4,64,8,128]{3,2,1,0:T(8,128)} %copy-done.1, f32[8,128]{1,0:T(8,128)} %kern_ref.1, bf16[256,256]{1,0:T(8,128)(2,1)} %fusion.3.f1_ref, f32[2,64,128]{2,1,0:T(8,128)} %pad_maximum_fusion.4.tw_ref, ...), custom_call_target="tpu_custom_call" | custom-call | tf_op jit(solution)/shard_map/grid_rows/pallas_call | solution.py:197
  199.2 24.3 %all-to-all-start.1 = ((f32[16,136,8,128]{3,2,1,0:T(8,128)}), f32[16,136,8,128]{3,2,1,0:T(8,128)}, u32[]{:S(2)}, u32[]{:S(2)}) async-start(f32[16,136,8,128]{3,2,1,0:T(8,128)} %grid_rows.1), calls=%async_computation.1 | async-start | bytes 17825792 | tf_op jit(solution)/shard_map/all_to_all | solution.py:382
  223.6 0.1 add.144
  223.7 0.2 negate_select_fusion.10
  223.8 0.1 reduce-precision_convert_fusion.3
  223.9 0.6 fusion.6.e2_ref
  224.5 0.2 fusion.49
  224.8 0.1 pad_maximum_fusion.2
  224.9 0.6 fusion.2
  225.5 0.7 pad_maximum_fusion.3.f2_ref
  226.2 104.4 %all-to-all-done.1.h_ref = f32[16,136,8,128]{3,2,1,0:T(8,128)} async-done(((f32[16,136,8,128]{3,2,1,0:T(8,128)}), f32[16,136,8,128]{3,2,1,0:T(8,128)}, u32[]{:S(2)}, u32[]{:S(2)}) %all-to-all-start.1) | async-done | bytes 8912928 | tf_op jit(solution)/shard_map/all_to_all | solution.py:382
  330.6 33.5 %columns.1 = f32[256,8192]{1,0:T(8,128)} custom-call(s32[2]{0:T(128)} %add_convert_fusion.flags_ref, f32[16,136,8,128]{3,2,1,0:T(8,128)} %all-to-all-done.1.h_ref, bf16[256,256]{1,0:T(8,128)(2,1)} %pad_maximum_fusion.3.f2_ref, bf16[128,256]{1,0:T(8,128)(2,1)} %get-tuple-element.5.f2l_ref, f32[2,64,128]{2,1,0:T(8,128)} %pad_maximum_fusion.4.tw_ref, ...), custom_call_target="tpu_custom_call" | custom-call | tf_op jit(solution)/shard_map/columns/pallas_call | solution.py:317
  (11 shorter events, 0.1 us)
Async XLA Ops:
  5.0 18.8 %all-to-all-start = ((f32[4,4,16,8,128]{4,3,2,1,0:T(8,128)}), f32[4,4,16,8,128]{4,3,2,1,0:T(8,128)S(1)}, u32[]{:S(2)}, u32[]{:S(2)}) async-start(f32[4,4,16,8,128]{4,3,2,1,0:T(8,128)} %bitcast.2), calls=%async_computation | async-start | bytes 2097152 | tf_op jit(solution)/shard_map/all_to_all | solution.py:365
  23.9 28.7 %copy-start = (f32[1,4,4,16,8,128]{5,4,3,2,1,0:T(8,128)}, f32[1,4,4,16,8,128]{5,4,3,2,1,0:T(8,128)S(1)}, u32[]{:S(2)}) copy-start(f32[1,4,4,16,8,128]{5,4,3,2,1,0:T(8,128)S(1)} %copy.13) | copy-start | bytes 3145732
  23.9 28.7 %collective-permute-start = (f32[4,64,8,128]{3,2,1,0:T(8,128)S(1)}, f32[4,64,8,128]{3,2,1,0:T(8,128)S(1)}, u32[]{:S(2)}, u32[]{:S(2)}) collective-permute-start(f32[4,64,8,128]{3,2,1,0:T(8,128)S(1)} %bitcast.35), channel_id=1, source_target_pairs={{0,31},{1,30},{2,29},{3,28},{4,27},{5,26},{6,25},{7,24},{8,23},{9,... | collective-permute-start | bytes 3145736 | tf_op jit(solution)/shard_map/ppermute | solution.py:367
  28.7 23.9 %copy-start.2 = (bf16[128,256]{1,0:T(8,128)(2,1)}, bf16[128,256]{1,0:T(8,128)(2,1)S(1)}, u32[]{:S(2)}) copy-start(bf16[128,256]{1,0:T(8,128)(2,1)S(1)} %get-tuple-element.7.el_ref) | copy-start | bytes 196612
  52.6 1.0 copy-start.1
  199.2 131.3 %all-to-all-start.1 = ((f32[16,136,8,128]{3,2,1,0:T(8,128)}), f32[16,136,8,128]{3,2,1,0:T(8,128)}, u32[]{:S(2)}, u32[]{:S(2)}) async-start(f32[16,136,8,128]{3,2,1,0:T(8,128)} %grid_rows.1), calls=%async_computation.1 | async-start | bytes 17825792 | tf_op jit(solution)/shard_map/all_to_all | solution.py:382

commit v2 on v1

--- a/solution.py
+++ b/solution.py
@@ -74,156 +74,166 @@
         hi = x.astype(BF16).astype(F32)
         return hi, x - hi
 
-    row_hi, row_lo = halves(rows)
     row_masks = [row_block == j for j in range(PATCH // SUB + 2)]
-    a_hi = jnp.concatenate([jnp.where(m, row_hi, 0.0) for m in row_masks], axis=0).astype(BF16)
-    a_lo = jnp.concatenate([jnp.where(m, row_lo, 0.0) for m in row_masks], axis=0).astype(BF16)
+    a_hi, a_lo = [], []
+    for value in (values_re, values_im):
+        hi, lo = halves(rows * value)
+        a_hi += [jnp.where(m, hi, 0.0) for m in row_masks]
+        a_lo += [jnp.where(m, lo, 0.0) for m in row_masks]
+    col_hi, col_lo = halves(cols)
     col_masks = [col_block == j for j in range(2 * PATCH // SUB)]
     live = [(j - parity * (PATCH // SUB)) % len(col_masks) in (*range(9), 15) for j in range(len(col_masks))]
     zero = jnp.zeros_like(cols)
-    b_hi, b_lo = [], []
-    for value in (values_re, values_im):
-        hi, lo = halves(cols * value)
-        b_hi += [jnp.where(m, hi, 0.0) if on else zero for m, on in zip(col_masks, live)]
-        b_lo += [jnp.where(m, lo, 0.0) if on else zero for m, on in zip(col_masks, live)]
-    return a_hi, a_lo, jnp.concatenate(b_hi, axis=0).astype(BF16), jnp.concatenate(b_lo, axis=0).astype(BF16)
+    b = [jnp.where(m, x, 0.0) if on else zero for x in (col_hi, col_lo) for m, on in zip(col_masks, live)]
+    return jnp.concatenate(a_hi + a_lo, axis=0).astype(BF16), jnp.concatenate(b, axis=0).astype(BF16)
 
 
 def tile_of(kern, low, high, parity, length):
-    la_hi, la_lo, lb_hi, lb_lo = patch_operands(kern, low, False, parity, length)
-    ha_hi, ha_lo, hb_hi, hb_lo = patch_operands(kern, high, True, parity, length)
-    a_hi = jnp.concatenate([la_hi, ha_hi], axis=1)
-    a_lo = jnp.concatenate([la_lo, ha_lo], axis=1)
-    b_hi = jnp.concatenate([lb_hi, hb_hi], axis=1)
-    b_lo = jnp.concatenate([lb_lo, hb_lo], axis=1)
-    rows = a_hi.shape[0]
-    main = dot_nt(jnp.concatenate([a_hi, a_lo], axis=0), b_hi)
-    return main[:rows] + main[rows:] + dot_nt(a_hi, b_lo)
-
-
-def grid_kernel(dims, flags_ref, own_ref, par_ref, kern_ref, f1_ref, tw_ref, eh_ref, el_ref, h_ref, g_ref, carry_ref):
-    bands, pairs, row_stride, length = dims
-    tile_rows = PATCH + 2 * SUB
-    is_low = flags_ref[0] == 1
-    is_last = flags_ref[1] == 1
+    low_a, low_b = patch_operands(kern, low, False, parity, length)
+    high_a, high_b = patch_operands(kern, high, True, parity, length)
+    a = jnp.concatenate([low_a, high_a], axis=1)
+    b = jnp.concatenate([low_b, high_b], axis=1)
+    rows = a.shape[0] // 2
+    out = dot_nt(a, b)
+    return out[:rows, :LANES] + out[:rows, LANES:] + out[rows:, :LANES]
+
+
+def grid_kernel(dims, *refs):
+    pairs, row_stride, length, first_band, last_band = dims
+    last_ref, low_ref, high_ref, kern_ref, f1_ref, tw_ref, eh_ref, el_ref = refs[:8]
+    refs = refs[8:]
+    if not first_band:
+        in_ref, refs = refs[0], refs[1:]
+    h_ref, refs = refs[0], refs[1:]
+    if not last_band:
+        out_ref, refs = refs[0], refs[1:]
+    g_ref, carry_ref = refs
+    spill = 2 * SUB
+    tile_rows = PATCH + spill
+    rows = tile_rows if last_band else PATCH
+    is_last = last_ref[0] == 1
     kern = kern_ref[...]
     parts = 2 * pairs
-    lane = lax.broadcasted_iota(jnp.int32, (tile_rows, 2 * LANES), 1) & (LANES - 1)
-
-    def clear(n, _):
+    lane = lax.broadcasted_iota(jnp.int32, (2 * tile_rows, LANES), 1)
+
+    def columns(q):
+        nxt = jnp.where(q == pairs - 1, 0, q + 1)
+        odd = tile_of(kern, low_ref[q, 4:8, :], high_ref[pairs - 1 - q, 0:4, :], 1, length)
+        even = tile_of(kern, low_ref[nxt, 0:4, :], high_ref[pairs - 1 - nxt, 4:8, :], 0, length)
+        here = jnp.where(lane < SUB, 0.0, odd) + jnp.where(lane < LANES - SUB, 0.0, even)
+        there = jnp.where(lane < SUB, odd, 0.0) + jnp.where(lane < LANES - SUB, even, 0.0)
+        return here, there
+
+    _, there = columns(pairs - 1)
+    carry_ref[...] = there
+
+    def step(q, _):
+        here, there = columns(q)
+        total = here + carry_ref[...]
+        carry_ref[...] = there
         for part in range(2):
-            base = pl.multiple_of((part * pairs + n) * row_stride, SUB)
-            g_ref[pl.ds(base, row_stride), :] = jnp.zeros((row_stride, LANES), F32)
+            value = total[part * tile_rows : (part + 1) * tile_rows]
+            at = part * pairs + q
+            base = pl.multiple_of(at * row_stride, SUB)
+            shared = pl.ds(pl.multiple_of(at * spill, SUB), spill)
+            top = value[:spill]
+            if not first_band:
+                top = top + in_ref[shared, :]
+            g_ref[pl.ds(base, spill), :] = top
+            g_ref[pl.ds(base + spill, rows - spill), :] = value[spill:rows]
+            if not last_band:
+                out_ref[shared, :] = value[rows:]
         return 0
 
-    lax.fori_loop(0, pairs, clear, 0)
-
-    for band in range(bands):
-
-        def fields_at(q, parity):
-            own_low = own_ref[band, q, 4 * parity : 4 * parity + 4, :]
-            par_low = par_ref[band, q, 4 * parity : 4 * parity + 4, :]
-            mq = pairs - 1 - q
-            mp = 1 - parity
-            own_high = own_ref[bands - 1 - band, mq, 4 * mp : 4 * mp + 4, :]
-            par_high = par_ref[bands - 1 - band, mq, 4 * mp : 4 * mp + 4, :]
-            return jnp.where(is_low, own_low, par_low), jnp.where(is_low, par_high, own_high)
-
-        def columns(q):
-            odd = tile_of(kern, *fields_at(q, 1), 1, length)
-            nxt = jnp.where(q == pairs - 1, 0, q + 1)
-            even = tile_of(kern, *fields_at(nxt, 0), 0, length)
-            here = jnp.where(lane < SUB, 0.0, odd) + jnp.where(lane < LANES - SUB, 0.0, even)
-            there = jnp.where(lane < SUB, odd, 0.0) + jnp.where(lane < LANES - SUB, even, 0.0)
-            return here, there
-
-        _, there = columns(pairs - 1)
-        carry_ref[...] = there
-
-        def step(q, _):
-            here, there = columns(q)
-            total = here + carry_ref[...]
-            carry_ref[...] = there
-            for part in range(2):
-                base = pl.multiple_of((part * pairs + q) * row_stride, SUB) + band * PATCH
-                where = pl.ds(base, tile_rows)
-                g_ref[where, :] = g_ref[where, :] + total[:, part * LANES : (part + 1) * LANES]
-            return 0
-
-        lax.fori_loop(0, pairs, step, 0)
-
-        cos = tw_ref[0]
-        sin = tw_ref[1]
-
-        def quad(group, _):
-            first = band * PATCH + 4 * group
-            lines = []
-            for pair in range(2):
-                cells = []
-                for one in range(2):
-                    row = first + 2 * pair + one
-                    up = bands * PATCH + SUB
-                    j = row - up
+    lax.fori_loop(0, pairs, step, 0, unroll=GRID_UNROLL)
+
+    cos = tw_ref[0]
+    sin = tw_ref[1]
+
+    def quad(group, _):
+        lines = []
+        for pair in range(2):
+            cells = []
+            for one in range(2):
+                row = 4 * group + 2 * pair + one
+                if last_band:
+                    j = row - PATCH - SUB
                     moved = jnp.where(j == 6, 0, jnp.where(j == 7, 7, jnp.where(j % 2 == 0, j + 2, j)))
-                    row = jnp.where(is_last & (j >= 0), up + moved, row)
-                    cells.append(g_ref[pl.ds(row, parts, stride=row_stride), :])
-                hi, lo = split(jnp.concatenate(cells, axis=1))
-                out = dot(f1_ref[...], jnp.concatenate([hi, lo], axis=0))
-                out = out[:parts] + out[parts:]
-                for one in range(2):
-                    re = out[:pairs, one * LANES : (one + 1) * LANES]
-                    im = out[pairs:, one * LANES : (one + 1) * LANES]
-                    lines.append(jnp.concatenate([re * cos - im * sin, re * sin + im * cos], axis=1))
-            hi, lo = split(jnp.concatenate(lines, axis=0))
-            count = el_ref.shape[0]
-            out = dot_nt(eh_ref[...], hi)
-            out = out[:count] + out[count:] + dot_nt(el_ref[...], lo)
-            dests, _, share, _ = h_ref.shape
-            for part in range(2):
-                piece = out[:, part * LANES : (part + 1) * LANES].reshape(dests, share, LANES)
-                h_ref[:, first // 2 + part, :, :] = piece
-            return 0
-
-        groups = PATCH // 4 + (2 * SUB // 4 if band == bands - 1 else 0)
-        lax.fori_loop(0, groups, quad, 0)
-
-
-def grid_and_rows(flags, own, par, kern, f1, tw, eh, el, dests, length):
-    bands, pairs = own.shape[0], own.shape[1]
-    rows = bands * PATCH + 2 * SUB
+                    row = jnp.where(is_last & (j >= 0), PATCH + SUB + moved, row)
+                cells.append(g_ref[pl.ds(row, parts, stride=row_stride), :])
+            hi, lo = split(jnp.concatenate(cells, axis=1))
+            out = dot(f1_ref[...], jnp.concatenate([hi, lo], axis=0))
+            out = out[:parts] + out[parts:]
+            for one in range(2):
+                re = out[:pairs, one * LANES : (one + 1) * LANES]
+                im = out[pairs:, one * LANES : (one + 1) * LANES]
+                lines.append(jnp.concatenate([re * cos - im * sin, re * sin + im * cos], axis=1))
+        hi, lo = split(jnp.concatenate(lines, axis=0))
+        count = el_ref.shape[0]
+        out = dot_nt(eh_ref[...], hi)
+        out = out[:count] + out[count:] + dot_nt(el_ref[...], lo)
+        dests, _, share, _ = h_ref.shape
+        for part in range(2):
+            piece = out[:, part * LANES : (part + 1) * LANES].reshape(dests, share, LANES)
+            h_ref[:, 2 * group + part, :, :] = piece
+        return 0
+
+    lax.fori_loop(0, rows // 4, quad, 0, unroll=QUAD_UNROLL)
+
+
+GRID_UNROLL = 8
+QUAD_UNROLL = 8
+
+
+def grid_and_rows(last, low, high, kern, tables, carry, dests, length, last_band):
+    pairs = low.shape[0]
+    spill = 2 * SUB
+    rows = PATCH + spill if last_band else PATCH
     row_stride = rows + SUB
-    outs = el.shape[0]
+    outs = tables[3].shape[0]
+    shared = (2 * pairs * spill, LANES)
     vmem = pl.BlockSpec(memory_space=pltpu.VMEM)
-    return pl.pallas_call(
-        functools.partial(grid_kernel, (bands, pairs, row_stride, length)),
-        out_shape=jax.ShapeDtypeStruct((dests, rows * pairs // LANES, outs // dests, LANES), F32),
-        in_specs=[pl.BlockSpec(memory_space=pltpu.SMEM)] + [vmem] * 7,
-        out_specs=vmem,
+    out_shape = [jax.ShapeDtypeStruct((dests, rows * pairs // LANES, outs // dests, LANES), F32)]
+    if not last_band:
+        out_shape.append(jax.ShapeDtypeStruct(shared, F32))
+    args = [low, high, kern, *tables] + ([] if carry is None else [carry])
+    out = pl.pallas_call(
+        functools.partial(grid_kernel, (pairs, row_stride, length, carry is None, last_band)),
+        out_shape=out_shape,
+        in_specs=[pl.BlockSpec(memory_space=pltpu.SMEM)] + [vmem] * len(args),
+        out_specs=[vmem] * len(out_shape),
         scratch_shapes=[
             pltpu.VMEM((2 * pairs * row_stride, LANES), F32),
-            pltpu.VMEM((PATCH + 2 * SUB, 2 * LANES), F32),
+            pltpu.VMEM((2 * (PATCH + spill), LANES), F32),
         ],
-        compiler_params=pltpu.CompilerParams(vmem_limit_bytes=60 * 1024 * 1024),
+        compiler_params=pltpu.CompilerParams(vmem_limit_bytes=40 * 1024 * 1024),
+        cost_estimate=pl.CostEstimate(flops=20 * 10**9, bytes_accessed=8 * 2**20, transcendentals=0),
         name="grid_rows",
-    )(flags, own, par, kern, f1, tw, eh, el)
-
-
-def column_kernel(dims, flags_ref, h_ref, f2_ref, f2l_ref, tw_ref, e2_ref, out_ref, r_ref, z_ref, s_ref, sems):
+    )(last, *args)
+    return out if not last_band else (out[0], None)
+
+
+def column_kernel(dims, flags_ref, *refs):
     sources, spans, bands, block_rows = dims
+    h_refs = refs[:bands]
+    f2_ref, f2l_ref, tw_ref, e2_ref, out_ref, r_ref, z_ref, s_ref, sems = refs[bands:]
     share = 2 * spans
     low = flags_ref[0] == 1
     width = LANES
     y_count = spans * PATCH
     half = PATCH // 2
 
-    blocks = h_ref.shape[1]
+    blocks = sum(ref.shape[1] for ref in h_refs)
     stride = (blocks + 1) * share
 
     @pl.when(pl.program_id(0) == 0)
     def _():
         copies = [
-            pltpu.make_async_copy(h_ref.at[n], r_ref.at[pl.ds(n * (blocks + 1), blocks)], sems.at[n])
+            pltpu.make_async_copy(
+                ref.at[n], r_ref.at[pl.ds(n * (blocks + 1) + i * half, ref.shape[1])], sems.at[i * sources + n]
+            )
             for n in range(sources)
+            for i, ref in enumerate(h_refs)
         ]
         for copy in copies:
             copy.start()
@@ -310,7 +320,7 @@
     lax.fori_loop(0, block_rows // SUB, eight, 0)
 
 
-def columns_of(flags, h, f2, f2l, tw, e2, sources, spans, bands, length):
+def columns_of(flags, hs, f2, f2l, tw, e2, sources, spans, bands, length):
     y_count = spans * PATCH
     block_rows = min(32, y_count)
     vmem = pl.BlockSpec(memory_space=pltpu.VMEM)
@@ -318,17 +328,17 @@
         functools.partial(column_kernel, (sources, spans, bands, block_rows)),
         grid=(y_count // block_rows,),
         out_shape=jax.ShapeDtypeStruct((y_count, length), F32),
-        in_specs=[pl.BlockSpec(memory_space=pltpu.SMEM), pl.BlockSpec(memory_space=pl.ANY)] + [vmem] * 4,
+        in_specs=[pl.BlockSpec(memory_space=pltpu.SMEM)] + [pl.BlockSpec(memory_space=pl.ANY)] * bands + [vmem] * 4,
         out_specs=pl.BlockSpec((block_rows, length), lambda n: (n, 0)),
         scratch_shapes=[
-            pltpu.VMEM((sources * (h.shape[1] + 1), h.shape[2], LANES), F32),
+            pltpu.VMEM((sources * (sum(h.shape[1] for h in hs) + 1), hs[0].shape[2], LANES), F32),
             pltpu.VMEM((2 * PATCH * y_count, LANES), F32),
             pltpu.VMEM((PATCH * SUB, LANES), F32),
-            pltpu.SemaphoreType.DMA((sources,)),
+            pltpu.SemaphoreType.DMA((sources * bands,)),
         ],
         compiler_params=pltpu.CompilerParams(vmem_limit_bytes=60 * 1024 * 1024),
         name="columns",
-    )(flags, h, f2, f2l, tw, e2)
+    )(flags, *hs, f2, f2l, tw, e2)
 
 
 def split_table(x):
@@ -343,7 +353,6 @@
 
 def local(vis_value, vis_pos, counts, kernel, *, au, vert):
     devices = au * vert
-    half_au = au // 2
     axes = ("half", "sub", "vert")
     me = lax.axis_index(axes)
     low = me < devices // 2
@@ -364,10 +373,15 @@
     fields = fields.reshape(vert, bands, local_cols // 2, 8, slots)
     own = lax.all_to_all(fields, "vert", split_axis=0, concat_axis=2, tiled=True)
     own = own.reshape(bands, pairs, 8, slots)
-    par = lax.ppermute(own, axes, [(d, devices - 1 - d) for d in range(devices)])
+    mirror = [(d, devices - 1 - d) for d in range(devices)]
+    sent = jnp.where(low, own, own[::-1])
+    received = [lax.ppermute(sent[:1], axes, mirror)]
+    if bands > 1:
+        received.append(lax.ppermute(sent[1:], axes, mirror))
 
     band_index = jnp.where(low, me, devices - 1 - me)
-    flags = jnp.stack([low, band_index == sources - 1]).astype(jnp.int32)
+    flags = low.astype(jnp.int32)[None]
+    last = (band_index == sources - 1).astype(jnp.int32)[None]
 
     ya = jnp.arange(pairs, dtype=jnp.int32)
     p = jnp.arange(LANES, dtype=jnp.int32)
@@ -378,8 +392,16 @@
     second = real_parts(*turn(yb[:, None] * p[None, :], LANES))
     second = second.transpose(2, 0, 1, 3).reshape(LANES, 2 * LANES)
     hi, lo = split_table(second)
-    h = grid_and_rows(flags, own, par, kernel, f1, tw1, jnp.concatenate([hi, lo], axis=0), hi, sources, length)
-    h = lax.all_to_all(h, ("sub", "vert"), split_axis=0, concat_axis=0, tiled=True)
+    tables = (f1, tw1, jnp.concatenate([hi, lo], axis=0), hi)
+    carry, hs = None, []
+    for band in range(bands):
+        got = received[0][0] if band == 0 else received[1][band - 1]
+        low_patches = jnp.where(low, own[band], got)
+        high_patches = jnp.where(low, got, own[bands - 1 - band])
+        h, carry = grid_and_rows(
+            last, low_patches, high_patches, kernel, tables, carry, sources, length, band == bands - 1
+        )
+        hs.append(lax.all_to_all(h, ("sub", "vert"), split_axis=0, concat_axis=0, tiled=True))
 
     order = jnp.arange(sources, dtype=jnp.int32)
     order = jnp.where(low, order, sources - 1 - order)
@@ -392,7 +414,7 @@
     cos, sin = turn(r[:, None] * r[None, :], PATCH)
     last = jnp.concatenate([cos, jnp.where(r[None, :] == 0, 1.0, -sin)], axis=1) * scale
     return columns_of(
-        flags, h, jnp.concatenate([hi, hi], axis=0), lo, tw2, stacked(last), sources, spans, bands, length
+        flags, hs, jnp.concatenate([hi, hi], axis=0), lo, tw2, stacked(last), sources, spans, bands, length
     )
 
 
@@ -401,8 +423,12 @@
     halves = Mesh(mesh.devices.reshape(2, au // 2, vert), ("half", "sub", "vert"))
     rows = ("half", "sub")
     in_specs = (P(rows, "vert", None, None), P(rows, "vert", None, None), P(rows, "vert"), P())
+
+    def program(*args):
+        return local(*args, au=au, vert=vert)
+
     return jax.shard_map(
-        functools.partial(local, au=au, vert=vert),
+        program,
         mesh=halves,
         in_specs=in_specs,
         out_specs=P((*rows, "vert"), None),

time: 368 us -> 265 us (0.72)
  Pallas kernels: 179 us -> 91.2 us
  waiting for transfers between devices: 140 us -> 122 us
    pallas_call x1 -> x4, Pallas kernels: 146 us -> 57.3 us  [grid_and_rows(): pl.pallas_call(functools.partial(grid_kernel, (pairs, row_stride, length,...]
    all_to_all x1 -> x4, waiting for transfers between devices: 104 us -> 53.1 us  [local(): lax.all_to_all(h, ('sub', 'vert'), split_axis=0, concat_axis=0, tiled=True)]
    ppermute x1 -> x2, waiting for transfers between devices: 22.5 us -> 56.9 us  [the longest x1 48.9 us: local(): received.append(lax.ppermute(sent[1:], axes, mirror))]
    ppermute x1 -> x2, starting transfers between devices: 3 us -> 8.99 us  [the longest x1 5.99 us: local(): received.append(lax.ppermute(sent[1:], axes, mirror))]
    all_to_all x1 -> x4, starting transfers between devices: 24.3 us -> 21.5 us  [local(): lax.all_to_all(h, ('sub', 'vert'), split_axis=0, concat_axis=0, tiled=True)]
  transfers between devices with their start and end apart: 3 -> 7, of which waited for: 3 -> 6; matrix products, arithmetic and copies ran while one was open for 2% -> 3% of each run, Pallas kernels for 0% -> 17%
where the time goes in v2:
time: 265 us; the launch traced here: 262 us
  waiting for transfers between devices  122 us (46%)
  Pallas kernels  91.2 us (34%)
  starting transfers between devices  35.7 us (13%)
  other arithmetic  10.3 us (4%)
  local copies, waits for them, and re-layouts  2.98 us (1%)
    pallas_call x4, Pallas kernels, grid_and_rows(): pl.pallas_call(functools.partial(grid_kernel, (pairs, row_stride, length,...  57.3 us
    all_to_all x4, waiting for transfers between devices, local(): lax.all_to_all(h, ('sub', 'vert'), split_axis=0, concat_axis=0, tiled=True)  53.1 us
    ppermute x1, waiting for transfers between devices, local(): received.append(lax.ppermute(sent[1:], axes, mirror))  48.9 us
    pallas_call x1, Pallas kernels, columns_of(): pl.pallas_call(functools.partial(column_kernel, (sources, spans, bands, b...  34 us
    all_to_all x4, starting transfers between devices, local(): lax.all_to_all(h, ('sub', 'vert'), split_axis=0, concat_axis=0, tiled=True)  21.5 us
    all_to_all x1, waiting for transfers between devices, local(): lax.all_to_all(fields, 'vert', split_axis=0, concat_axis=2, tiled=True)  11.8 us
    ppermute x1, waiting for transfers between devices, local(): received = [lax.ppermute(sent[:1], axes, mirror)]  7.91 us
    ppermute x1, starting transfers between devices, local(): received.append(lax.ppermute(sent[1:], axes, mirror))  5.99 us
  transfers between devices with their start and end apart: 7, of which 6 were waited for; matrix products, arithmetic and copies ran while one was open for 3% of the time, Pallas kernels for 17%

profile of v2, /device:TPU:0, one launch (start us, length us, event | category | flops | bytes accessed | tf_op | source)
XLA Modules:
  0.0 262.4 jit_solution(2179284934365598480)
XLA Ops:
  0.0 0.8 iota_compare_fusion.1
  0.8 1.3 convert_element_type.111
  2.1 1.4 broadcast_select_fusion
  3.5 1.5 pad_maximum_fusion
  5.0 5.2 %all-to-all-start = ((f32[4,4,16,8,128]{4,3,2,1,0:T(8,128)}), f32[4,4,16,8,128]{4,3,2,1,0:T(8,128)S(1)}, u32[]{:S(2)}, u32[]{:S(2)}) async-start(f32[4,4,16,8,128]{4,3,2,1,0:T(8,128)} %bitcast.2), calls=%async_computation | async-start | bytes 2097152 | tf_op jit(solution)/shard_map/all_to_all | solution.py:374
  10.2 0.1 fusion.47
  10.3 0.1 fusion.45
  10.5 0.1 copy.14
  10.6 0.1 reshape.460
  10.8 0.2 fusion.48
  11.0 0.1 copy.15
  11.1 0.8 fusion.41
  12.0 11.8 %all-to-all-done = f32[4,4,16,8,128]{4,3,2,1,0:T(8,128)S(1)} async-done(((f32[4,4,16,8,128]{4,3,2,1,0:T(8,128)}), f32[4,4,16,8,128]{4,3,2,1,0:T(8,128)S(1)}, u32[]{:S(2)}, u32[]{:S(2)}) %all-to-all-start) | async-done | bytes 1048608 | tf_op jit(solution)/shard_map/all_to_all | solution.py:374
  23.8 0.1 copy.13
  23.9 0.1 reverse_select_fusion
  24.0 0.0 copy-start.1
  24.0 3.0 %collective-permute-start = (f32[1,64,8,128]{3,2,1,0:T(8,128)S(1)}, f32[1,64,8,128]{3,2,1,0:T(8,128)S(1)}, u32[]{:S(2)}, u32[]{:S(2)}) collective-permute-start(f32[1,64,8,128]{3,2,1,0:T(8,128)S(1)} %slice.45), channel_id=1, source_target_pairs={{0,31},{1,30},{2,29},{3,28},{4,27},{5,26},{6,25},{7,24},{8,23},{9,... | collective-permute-start | bytes 786440 | tf_op jit(solution)/shard_map/ppermute | solution.py:378
  27.0 0.0 copy-done.5
  27.0 0.0 copy-done.6
  27.0 0.0 copy-start
  27.1 0.9 fusion.51
  27.9 7.9 %collective-permute-done = f32[1,64,8,128]{3,2,1,0:T(8,128)S(1)} collective-permute-done((f32[1,64,8,128]{3,2,1,0:T(8,128)S(1)}, f32[1,64,8,128]{3,2,1,0:T(8,128)S(1)}, u32[]{:S(2)}, u32[]{:S(2)}) %collective-permute-start) | collective-permute-done | bytes 262176 | tf_op jit(solution)/shard_map/ppermute | solution.py:378
  35.9 13.6 %grid_rows.4 = (f32[16,32,8,128]{3,2,1,0:T(8,128)}, f32[2048,128]{1,0:T(8,128)S(1)}) custom-call(s32[1]{0:T(128)} %bitcast.1.refs_0_, f32[64,8,128]{2,1,0:T(8,128)S(1)} %get-tuple-element.30.refs_1_, f32[64,8,128]{2,1,0:T(8,128)S(1)} %get-tuple-element.29.refs_2_, f32[8,128]{1,0:T(8,128)S(1)} %copy-done.1, bf16[256,256]{1,0:T(8,128)(2,1)S(1)} %fusion.3.refs_4_, ...), custom_call_target="tpu_custom_call" | custom-call | flops 20000000000 | bytes 8388608 | tf_op jit(solution)/shard_map/grid_rows/pallas_call | solution.py:200
  49.5 7.4 %all-to-all-start.1 = ((f32[16,32,8,128]{3,2,1,0:T(8,128)}), f32[16,32,8,128]{3,2,1,0:T(8,128)}, u32[]{:S(2)}, u32[]{:S(2)}) async-start(f32[16,32,8,128]{3,2,1,0:T(8,128)} %get-tuple-element.11), calls=%async_computation.1 | async-start | bytes 4194304 | tf_op jit(solution)/shard_map/all_to_all | solution.py:404
  57.0 0.1 slice.48
  57.1 6.0 %collective-permute-start.1 = (f32[3,64,8,128]{3,2,1,0:T(8,128)S(1)}, f32[3,64,8,128]{3,2,1,0:T(8,128)S(1)}, u32[]{:S(2)}, u32[]{:S(2)}) collective-permute-start(f32[3,64,8,128]{3,2,1,0:T(8,128)S(1)} %slice.48), channel_id=1, source_target_pairs={{0,31},{1,30},{2,29},{3,28},{4,27},{5,26},{6,25},{7,24},{8,23},{9,... | collective-permute-start | bytes 2359304 | tf_op jit(solution)/shard_map/ppermute | solution.py:380
  63.0 48.9 %collective-permute-done.1 = f32[3,64,8,128]{3,2,1,0:T(8,128)S(1)} collective-permute-done((f32[3,64,8,128]{3,2,1,0:T(8,128)S(1)}, f32[3,64,8,128]{3,2,1,0:T(8,128)S(1)}, u32[]{:S(2)}, u32[]{:S(2)}) %collective-permute-start.1) | collective-permute-done | bytes 786464 | tf_op jit(solution)/shard_map/ppermute | solution.py:380
  112.0 1.3 bitcast_select_fusion.2
  113.3 13.7 %grid_rows.5 = (f32[16,32,8,128]{3,2,1,0:T(8,128)}, f32[2048,128]{1,0:T(8,128)S(1)}) custom-call(s32[1]{0:T(128)} %bitcast.1.refs_0_, f32[64,8,128]{2,1,0:T(8,128)S(1)} %get-tuple-element.18.refs_1_, f32[64,8,128]{2,1,0:T(8,128)S(1)} %get-tuple-element.27.refs_2_, f32[8,128]{1,0:T(8,128)S(1)} %copy-done.1, bf16[256,256]{1,0:T(8,128)(2,1)S(1)} %fusion.3.refs_4_, ...), custom_call_target="tpu_custom_call" | custom-call | flops 20000000000 | bytes 8388608 | tf_op jit(solution)/shard_map/grid_rows/pallas_call | solution.py:200
  127.0 0.0 all-to-all-done.1.refs_0_
  127.0 5.2 %all-to-all-start.2 = ((f32[16,32,8,128]{3,2,1,0:T(8,128)}), f32[16,32,8,128]{3,2,1,0:T(8,128)}, u32[]{:S(2)}, u32[]{:S(2)}) async-start(f32[16,32,8,128]{3,2,1,0:T(8,128)} %get-tuple-element.13), calls=%async_computation.2 | async-start | bytes 4194304 | tf_op jit(solution)/shard_map/all_to_all | solution.py:404
  132.2 13.7 %grid_rows.6 = (f32[16,32,8,128]{3,2,1,0:T(8,128)}, f32[2048,128]{1,0:T(8,128)S(1)}) custom-call(s32[1]{0:T(128)} %bitcast.1.refs_0_, f32[64,8,128]{2,1,0:T(8,128)S(1)} %get-tuple-element.28.refs_1_, f32[64,8,128]{2,1,0:T(8,128)S(1)} %get-tuple-element.17.refs_2_, f32[8,128]{1,0:T(8,128)S(1)} %copy-done.1, bf16[256,256]{1,0:T(8,128)(2,1)S(1)} %fusion.3.refs_4_, ...), custom_call_target="tpu_custom_call" | custom-call | flops 20000000000 | bytes 8388608 | tf_op jit(solution)/shard_map/grid_rows/pallas_call | solution.py:200
  145.9 13.1 %all-to-all-done.2.refs_1_ = f32[16,32,8,128]{3,2,1,0:T(8,128)} async-done(((f32[16,32,8,128]{3,2,1,0:T(8,128)}), f32[16,32,8,128]{3,2,1,0:T(8,128)}, u32[]{:S(2)}, u32[]{:S(2)}) %all-to-all-start.2) | async-done | bytes 2097184 | tf_op jit(solution)/shard_map/all_to_all | solution.py:404
  159.0 4.6 %all-to-all-start.3 = ((f32[16,32,8,128]{3,2,1,0:T(8,128)}), f32[16,32,8,128]{3,2,1,0:T(8,128)}, u32[]{:S(2)}, u32[]{:S(2)}) async-start(f32[16,32,8,128]{3,2,1,0:T(8,128)} %get-tuple-element.15), calls=%async_computation.3 | async-start | bytes 4194304 | tf_op jit(solution)/shard_map/all_to_all | solution.py:404
  163.6 16.3 %grid_rows.7 = f32[16,40,8,128]{3,2,1,0:T(8,128)} custom-call(s32[1]{0:T(128)} %bitcast.1.refs_0_, f32[64,8,128]{2,1,0:T(8,128)S(1)} %get-tuple-element.26.refs_1_, f32[64,8,128]{2,1,0:T(8,128)S(1)} %get-tuple-element.25.refs_2_, f32[8,128]{1,0:T(8,128)S(1)} %copy-done.1, bf16[256,256]{1,0:T(8,128)(2,1)S(1)} %fusion.3.refs_4_, ...), custom_call_target="tpu_custom_call" | custom-call | flops 20000000000 | bytes 8388608 | tf_op jit(solution)/shard_map/grid_rows/pallas_call | solution.py:200
  179.9 10.2 %all-to-all-done.3.refs_2_ = f32[16,32,8,128]{3,2,1,0:T(8,128)} async-done(((f32[16,32,8,128]{3,2,1,0:T(8,128)}), f32[16,32,8,128]{3,2,1,0:T(8,128)}, u32[]{:S(2)}, u32[]{:S(2)}) %all-to-all-start.3) | async-done | bytes 2097184 | tf_op jit(solution)/shard_map/all_to_all | solution.py:404
  190.1 4.3 %all-to-all-start.4 = ((f32[16,40,8,128]{3,2,1,0:T(8,128)}), f32[16,40,8,128]{3,2,1,0:T(8,128)S(1)}, u32[]{:S(2)}, u32[]{:S(2)}) async-start(f32[16,40,8,128]{3,2,1,0:T(8,128)} %grid_rows.7), calls=%async_computation.4 | async-start | bytes 5242880 | tf_op jit(solution)/shard_map/all_to_all | solution.py:404
  194.4 0.1 add.144
  194.5 0.2 negate_select_fusion.10
  194.6 0.1 reduce-precision_convert_fusion.3
  194.7 0.6 fusion.6.refs_7_
  195.4 0.2 fusion.49
  195.6 0.1 pad_maximum_fusion.2
  195.7 0.7 fusion.2
  196.4 0.7 pad_maximum_fusion.3.refs_4_
  197.1 29.7 %all-to-all-done.4.refs_3_ = f32[16,40,8,128]{3,2,1,0:T(8,128)S(1)} async-done(((f32[16,40,8,128]{3,2,1,0:T(8,128)}), f32[16,40,8,128]{3,2,1,0:T(8,128)S(1)}, u32[]{:S(2)}, u32[]{:S(2)}) %all-to-all-start.4) | async-done | bytes 2621472 | tf_op jit(solution)/shard_map/all_to_all | solution.py:404
  226.8 1.5 copy-done.2
  228.3 34.0 %columns.1 = f32[256,8192]{1,0:T(8,128)} custom-call(s32[1]{0:T(128)} %bitcast.flags_ref, f32[16,32,8,128]{3,2,1,0:T(8,128)} %all-to-all-done.1.refs_0_, f32[16,32,8,128]{3,2,1,0:T(8,128)} %all-to-all-done.2.refs_1_, f32[16,32,8,128]{3,2,1,0:T(8,128)} %all-to-all-done.3.refs_2_, f32[16,40,8,128]{3,2,1,0:T(8,128)} %copy-done.2, ...), custom_call_target="tpu_custom_call" | custom-call | tf_op jit(solution)/shard_map/columns/pallas_call | solution.py:327
  (25 shorter events, 0.2 us)
Async XLA Ops:
  5.0 18.8 %all-to-all-start = ((f32[4,4,16,8,128]{4,3,2,1,0:T(8,128)}), f32[4,4,16,8,128]{4,3,2,1,0:T(8,128)S(1)}, u32[]{:S(2)}, u32[]{:S(2)}) async-start(f32[4,4,16,8,128]{4,3,2,1,0:T(8,128)} %bitcast.2), calls=%async_computation | async-start | bytes 2097152 | tf_op jit(solution)/shard_map/all_to_all | solution.py:374
  23.8 3.2 %copy-start.5 = (f32[1,64,128]{2,1,0:T(8,128)S(1)}, f32[1,64,128]{2,1,0:T(8,128)}, u32[]{:S(2)}) copy-start(f32[1,64,128]{2,1,0:T(8,128)} %get-tuple-element.53) | copy-start | bytes 98308
  23.8 3.2 %copy-start.6 = (f32[1,64,128]{2,1,0:T(8,128)S(1)}, f32[1,64,128]{2,1,0:T(8,128)}, u32[]{:S(2)}) copy-start(f32[1,64,128]{2,1,0:T(8,128)} %get-tuple-element.54) | copy-start | bytes 98308
  24.0 11.9 %copy-start.1 = (f32[8,128]{1,0:T(8,128)S(1)}, f32[8,128]{1,0:T(8,128)}, u32[]{:S(2)}) copy-start(f32[8,128]{1,0:T(8,128)} %refs_3_.7) | copy-start | bytes 12292
  24.0 11.8 %collective-permute-start = (f32[1,64,8,128]{3,2,1,0:T(8,128)S(1)}, f32[1,64,8,128]{3,2,1,0:T(8,128)S(1)}, u32[]{:S(2)}, u32[]{:S(2)}) collective-permute-start(f32[1,64,8,128]{3,2,1,0:T(8,128)S(1)} %slice.45), channel_id=1, source_target_pairs={{0,31},{1,30},{2,29},{3,28},{4,27},{5,26},{6,25},{7,24},{8,23},{9,... | collective-permute-start | bytes 786440 | tf_op jit(solution)/shard_map/ppermute | solution.py:378
  27.0 136.6 %copy-start = (f32[2,64,128]{2,1,0:T(8,128)}, f32[2,64,128]{2,1,0:T(8,128)S(1)}, u32[]{:S(2)}) copy-start(f32[2,64,128]{2,1,0:T(8,128)S(1)} %pad_maximum_fusion.4.refs_5_.refs_6_) | copy-start | bytes 196612
  27.9 8.0 %copy-start.3 = (f32[1,1,4,16,8,128]{5,4,3,1,2,0:T(8,128)}, f32[1,1,4,16,8,128]{5,4,3,1,2,0:T(8,128)S(1)}, u32[]{:S(2)}) copy-start(f32[1,1,4,16,8,128]{5,4,3,1,2,0:T(8,128)S(1)} %get-tuple-element.23) | copy-start | bytes 786436
  27.9 8.0 %copy-start.4 = (f32[1,1,4,16,8,128]{5,4,3,1,2,0:T(8,128)}, f32[1,1,4,16,8,128]{5,4,3,1,2,0:T(8,128)S(1)}, u32[]{:S(2)}) copy-start(f32[1,1,4,16,8,128]{5,4,3,1,2,0:T(8,128)S(1)} %get-tuple-element.24) | copy-start | bytes 786436
  49.5 77.5 %all-to-all-start.1 = ((f32[16,32,8,128]{3,2,1,0:T(8,128)}), f32[16,32,8,128]{3,2,1,0:T(8,128)}, u32[]{:S(2)}, u32[]{:S(2)}) async-start(f32[16,32,8,128]{3,2,1,0:T(8,128)} %get-tuple-element.11), calls=%async_computation.1 | async-start | bytes 4194304 | tf_op jit(solution)/shard_map/all_to_all | solution.py:404
  57.1 54.9 %collective-permute-start.1 = (f32[3,64,8,128]{3,2,1,0:T(8,128)S(1)}, f32[3,64,8,128]{3,2,1,0:T(8,128)S(1)}, u32[]{:S(2)}, u32[]{:S(2)}) collective-permute-start(f32[3,64,8,128]{3,2,1,0:T(8,128)S(1)} %slice.48), channel_id=1, source_target_pairs={{0,31},{1,30},{2,29},{3,28},{4,27},{5,26},{6,25},{7,24},{8,23},{9,... | collective-permute-start | bytes 2359304 | tf_op jit(solution)/shard_map/ppermute | solution.py:380
  127.0 32.0 %all-to-all-start.2 = ((f32[16,32,8,128]{3,2,1,0:T(8,128)}), f32[16,32,8,128]{3,2,1,0:T(8,128)}, u32[]{:S(2)}, u32[]{:S(2)}) async-start(f32[16,32,8,128]{3,2,1,0:T(8,128)} %get-tuple-element.13), calls=%async_computation.2 | async-start | bytes 4194304 | tf_op jit(solution)/shard_map/all_to_all | solution.py:404
  159.0 31.1 %all-to-all-start.3 = ((f32[16,32,8,128]{3,2,1,0:T(8,128)}), f32[16,32,8,128]{3,2,1,0:T(8,128)}, u32[]{:S(2)}, u32[]{:S(2)}) async-start(f32[16,32,8,128]{3,2,1,0:T(8,128)} %get-tuple-element.15), calls=%async_computation.3 | async-start | bytes 4194304 | tf_op jit(solution)/shard_map/all_to_all | solution.py:404
  190.1 36.7 %all-to-all-start.4 = ((f32[16,40,8,128]{3,2,1,0:T(8,128)}), f32[16,40,8,128]{3,2,1,0:T(8,128)S(1)}, u32[]{:S(2)}, u32[]{:S(2)}) async-start(f32[16,40,8,128]{3,2,1,0:T(8,128)} %grid_rows.7), calls=%async_computation.4 | async-start | bytes 5242880 | tf_op jit(solution)/shard_map/all_to_all | solution.py:404
  226.8 1.5 copy-start.2

commit v3 on v2

--- a/solution.py
+++ b/solution.py
@@ -214,13 +214,13 @@
 
 
 def column_kernel(dims, flags_ref, *refs):
-    sources, spans, bands, block_rows = dims
+    sources, spans, bands, block_rows, vert = dims
     h_refs = refs[:bands]
-    f2_ref, f2l_ref, tw_ref, e2_ref, out_ref, r_ref, z_ref, s_ref, sems = refs[bands:]
+    f2_ref, f2l_ref, tw_ref, e2_ref, out_ref, r_ref, z_ref, s_ref = refs[bands:]
     share = 2 * spans
     low = flags_ref[0] == 1
     width = LANES
-    y_count = spans * PATCH
+    z_pitch = spans * PATCH + SUB
     half = PATCH // 2
 
     blocks = sum(ref.shape[1] for ref in h_refs)
@@ -228,24 +228,19 @@
 
     @pl.when(pl.program_id(0) == 0)
     def _():
-        copies = [
-            pltpu.make_async_copy(
-                ref.at[n], r_ref.at[pl.ds(n * (blocks + 1) + i * half, ref.shape[1])], sems.at[i * sources + n]
-            )
-            for n in range(sources)
-            for i, ref in enumerate(h_refs)
-        ]
-        for copy in copies:
-            copy.start()
-        for copy in copies:
-            copy.wait()
+        def arrived(n, _):
+            for i, ref in enumerate(h_refs):
+                r_ref[pl.ds(n * (blocks + 1) + i * half, ref.shape[1])] = ref[n]
+            return 0
+
+        lax.fori_loop(0, sources, arrived, 0)
         flat = r_ref.reshape(sources * stride, width)
         up_block = SUB // 2 + bands * half
         sub = lax.broadcasted_iota(jnp.int32, (share, width), 0)
         sign = jnp.where(sub % 2 == 0, 1.0, -1.0)
 
         def at_block(n, block):
-            source = jnp.where(low, n, sources - 1 - n)
+            source = jnp.where(low, n, backwards(n, vert, sources // vert))
             return source * (blocks + 1) + block
 
         def add(to, value):
@@ -281,7 +276,7 @@
             x = jnp.concatenate(tall, axis=0)
             hi, lo = split(x)
             z = dot(jnp.concatenate([hi, lo], axis=1), f2_ref[...]) + dot(hi, f2l_ref[...])
-            top_col = jnp.where(low, x[:, PATCH : PATCH + 1], x[:, PATCH + sources - 1 : PATCH + sources])
+            top_col = jnp.where(low, x[:, PATCH : PATCH + 1], x[:, PATCH + sources - vert : PATCH + sources - vert + 1])
             for k in range(spans):
                 for one in range(2):
                     at = (2 * k + one) * PATCH
@@ -295,18 +290,18 @@
                     if one == 0:
                         nyquist = flip * top_col[at : at + PATCH]
                         new_im = jnp.where(rho == 0, nyquist, new_im)
-                    z_ref[pl.ds(pl.multiple_of(line * y_count + k * PATCH, PATCH), PATCH), :] = new_re
-                    z_ref[pl.ds(pl.multiple_of((PATCH + line) * y_count + k * PATCH, PATCH), PATCH), :] = new_im
+                    z_ref[pl.ds(pl.multiple_of(line * z_pitch + k * PATCH, SUB), PATCH), :] = new_re
+                    z_ref[pl.ds(pl.multiple_of((PATCH + line) * z_pitch + k * PATCH, SUB), PATCH), :] = new_im
             return 0
 
-        lax.fori_loop(0, half, pair_step, 0)
+        lax.fori_loop(0, half, pair_step, 0, unroll=4)
 
     start = pl.program_id(0) * block_rows
 
     def eight(group, _):
         for pair in range(SUB // 2):
             y = start + group * SUB + 2 * pair
-            cells = [z_ref[pl.ds(y + one, 2 * PATCH, stride=y_count), :] for one in range(2)]
+            cells = [z_ref[pl.ds(y + one, 2 * PATCH, stride=z_pitch), :] for one in range(2)]
             hi, lo = split(jnp.concatenate(cells, axis=1))
             out = dot(e2_ref[...], jnp.concatenate([hi, lo], axis=0))
             out = out[:PATCH] + out[PATCH:]
@@ -317,24 +312,23 @@
             out_ref[at, block * width : (block + 1) * width] = s_ref[block * SUB : (block + 1) * SUB, :]
         return 0
 
-    lax.fori_loop(0, block_rows // SUB, eight, 0)
-
-
-def columns_of(flags, hs, f2, f2l, tw, e2, sources, spans, bands, length):
+    lax.fori_loop(0, block_rows // SUB, eight, 0, unroll=4)
+
+
+def columns_of(flags, hs, f2, f2l, tw, e2, sources, spans, bands, vert, length):
     y_count = spans * PATCH
     block_rows = min(32, y_count)
     vmem = pl.BlockSpec(memory_space=pltpu.VMEM)
     return pl.pallas_call(
-        functools.partial(column_kernel, (sources, spans, bands, block_rows)),
+        functools.partial(column_kernel, (sources, spans, bands, block_rows, vert)),
         grid=(y_count // block_rows,),
         out_shape=jax.ShapeDtypeStruct((y_count, length), F32),
-        in_specs=[pl.BlockSpec(memory_space=pltpu.SMEM)] + [pl.BlockSpec(memory_space=pl.ANY)] * bands + [vmem] * 4,
+        in_specs=[pl.BlockSpec(memory_space=pltpu.SMEM)] + [vmem] * (bands + 4),
         out_specs=pl.BlockSpec((block_rows, length), lambda n: (n, 0)),
         scratch_shapes=[
             pltpu.VMEM((sources * (sum(h.shape[1] for h in hs) + 1), hs[0].shape[2], LANES), F32),
-            pltpu.VMEM((2 * PATCH * y_count, LANES), F32),
+            pltpu.VMEM((2 * PATCH * (y_count + SUB), LANES), F32),
             pltpu.VMEM((PATCH * SUB, LANES), F32),
-            pltpu.SemaphoreType.DMA((sources * bands,)),
         ],
         compiler_params=pltpu.CompilerParams(vmem_limit_bytes=60 * 1024 * 1024),
         name="columns",
@@ -351,8 +345,13 @@
     return jnp.concatenate([jnp.concatenate([hi, hi], axis=1), jnp.concatenate([lo, jnp.zeros_like(lo)], axis=1)], axis=0)
 
 
+def backwards(n, vert, count):
+    return (count - 1 - n // vert) * vert + n % vert
+
+
 def local(vis_value, vis_pos, counts, kernel, *, au, vert):
     devices = au * vert
+    half_au = au // 2
     axes = ("half", "sub", "vert")
     me = lax.axis_index(axes)
     low = me < devices // 2
@@ -371,15 +370,17 @@
     live = jnp.arange(slots, dtype=jnp.int32) < counts[:, :, None, None]
     fields = jnp.concatenate([jnp.where(live, vis_value, 0.0), vis_pos.astype(F32)], axis=2)
     fields = fields.reshape(vert, bands, local_cols // 2, 8, slots)
+    fields = jnp.where(low, fields, fields[::-1])
     own = lax.all_to_all(fields, "vert", split_axis=0, concat_axis=2, tiled=True)
     own = own.reshape(bands, pairs, 8, slots)
-    mirror = [(d, devices - 1 - d) for d in range(devices)]
+    mirror = [(a * vert + v, (au - 1 - a) * vert + v) for a in range(au) for v in range(vert)]
     sent = jnp.where(low, own, own[::-1])
     received = [lax.ppermute(sent[:1], axes, mirror)]
     if bands > 1:
-        received.append(lax.ppermute(sent[1:], axes, mirror))
-
-    band_index = jnp.where(low, me, devices - 1 - me)
+        later, first_piece = lax.optimization_barrier((sent[1:], received[0]))
+        received = [first_piece, lax.ppermute(later, axes, mirror)]
+
+    band_index = jnp.where(low, me, lax.axis_index("vert") + vert * (au - 1 - me // vert))
     flags = low.astype(jnp.int32)[None]
     last = (band_index == sources - 1).astype(jnp.int32)[None]
 
@@ -404,7 +405,7 @@
         hs.append(lax.all_to_all(h, ("sub", "vert"), split_axis=0, concat_axis=0, tiled=True))
 
     order = jnp.arange(sources, dtype=jnp.int32)
-    order = jnp.where(low, order, sources - 1 - order)
+    order = jnp.where(low, order, backwards(order, vert, half_au))
     d = (bands * order[None, :] + jnp.arange(bands, dtype=jnp.int32)[:, None]).reshape(-1)
     xa = jnp.arange(LANES, dtype=jnp.int32)
     table = real_parts(*turn(xa[:, None] * d[None, :], LANES))
@@ -414,7 +415,7 @@
     cos, sin = turn(r[:, None] * r[None, :], PATCH)
     last = jnp.concatenate([cos, jnp.where(r[None, :] == 0, 1.0, -sin)], axis=1) * scale
     return columns_of(
-        flags, hs, jnp.concatenate([hi, hi], axis=0), lo, tw2, stacked(last), sources, spans, bands, length
+        flags, hs, jnp.concatenate([hi, hi], axis=0), lo, tw2, stacked(last), sources, spans, bands, vert, length
     )
 
 

time: 265 us -> 239 us (0.902)
  Pallas kernels: 91.2 us -> 76.2 us
  waiting for transfers between devices: 122 us -> 113 us
    pallas_call x1, Pallas kernels: 34 us -> 19 us  [columns_of(): pl.pallas_call(functools.partial(column_kernel, (sources, spans, bands, b...]
    ppermute x1, waiting for transfers between devices: 48.9 us -> 40.1 us  [local(): received = [first_piece, lax.ppermute(later, axes, mirror)]]
  transfers between devices with their start and end apart: 7 -> 7, of which waited for: 6 -> 6; matrix products, arithmetic and copies ran while one was open for 3% -> 2% of each run, Pallas kernels for 17% -> 18%
where the time goes in v3:
time: 239 us; the launch traced here: 236 us
  waiting for transfers between devices  113 us (47%)
  Pallas kernels  76.2 us (32%)
  starting transfers between devices  33.8 us (14%)
  other arithmetic  9.51 us (4%)
  local copies, waits for them, and re-layouts  3.76 us (2%)
    pallas_call x4, Pallas kernels, grid_and_rows(): pl.pallas_call(functools.partial(grid_kernel, (pairs, row_stride, length,...  57.3 us
    all_to_all x4, waiting for transfers between devices, local(): lax.all_to_all(h, ('sub', 'vert'), split_axis=0, concat_axis=0, tiled=True)  53.3 us
    ppermute x1, waiting for transfers between devices, local(): received = [first_piece, lax.ppermute(later, axes, mirror)]  40.1 us
    all_to_all x4, starting transfers between devices, local(): lax.all_to_all(h, ('sub', 'vert'), split_axis=0, concat_axis=0, tiled=True)  22.8 us
    pallas_call x1, Pallas kernels, columns_of(): pl.pallas_call(functools.partial(column_kernel, (sources, spans, bands, b...  19 us
    all_to_all x1, waiting for transfers between devices, local(): lax.all_to_all(fields, 'vert', split_axis=0, concat_axis=2, tiled=True)  12.4 us
    ppermute x1, waiting for transfers between devices, local(): received = [lax.ppermute(sent[:1], axes, mirror)]  7.02 us
    all_to_all x1, starting transfers between devices, local(): lax.all_to_all(fields, 'vert', split_axis=0, concat_axis=2, tiled=True)  5.19 us
  transfers between devices with their start and end apart: 7, of which 6 were waited for; matrix products, arithmetic and copies ran while one was open for 2% of the time, Pallas kernels for 18%

profile of v3, /device:TPU:0, one launch (start us, length us, event | category | flops | bytes accessed | tf_op | source)
XLA Modules:
  0.0 236.5 jit_solution(474258527798878210)
XLA Ops:
  0.0 0.8 iota_compare_fusion.1
  0.8 1.3 convert_element_type.111
  2.1 1.4 broadcast_select_fusion
  3.5 0.5 pad_maximum_fusion
  4.0 1.1 reverse_select_fusion.1
  5.1 5.2 %all-to-all-start = ((f32[4,4,16,8,128]{4,3,2,1,0:T(8,128)}), f32[4,4,16,8,128]{4,3,2,1,0:T(8,128)S(1)}, u32[]{:S(2)}, u32[]{:S(2)}) async-start(f32[4,4,16,8,128]{4,3,2,1,0:T(8,128)} %reverse_select_fusion.1), calls=%async_computation | async-start | bytes 2097152 | tf_op jit(solution)/shard_map/all_to_all | solution.py:374
  10.2 0.1 fusion.47
  10.4 0.1 fusion.45
  10.6 0.1 copy.16
  10.7 0.1 reshape.479
  10.8 0.2 fusion.48
  11.1 0.1 copy.17
  11.2 0.1 fusion.41
  11.4 12.4 %all-to-all-done = f32[4,4,16,8,128]{4,3,2,1,0:T(8,128)S(1)} async-done(((f32[4,4,16,8,128]{4,3,2,1,0:T(8,128)}), f32[4,4,16,8,128]{4,3,2,1,0:T(8,128)S(1)}, u32[]{:S(2)}, u32[]{:S(2)}) %all-to-all-start) | async-done | bytes 1048608 | tf_op jit(solution)/shard_map/all_to_all | solution.py:374
  23.9 0.1 copy.15
  24.0 0.1 reverse_select_fusion
  24.0 0.7 slice.46
  24.8 2.3 collective-permute-start
  27.1 1.0 slice.45
  28.1 0.1 fusion.54
  28.1 7.0 %collective-permute-done = f32[1,64,8,128]{3,2,1,0:T(8,128)} collective-permute-done((f32[1,64,8,128]{3,2,1,0:T(8,128)}, f32[1,64,8,128]{3,2,1,0:T(8,128)}, u32[]{:S(2)}, u32[]{:S(2)}) %collective-permute-start) | collective-permute-done | bytes 262176 | tf_op jit(solution)/shard_map/ppermute | solution.py:378
  35.2 1.0 bitcast_select_fusion.5
  36.2 0.0 copy-done.1
  36.2 13.6 %grid_rows.4 = (f32[16,32,8,128]{3,2,1,0:T(8,128)}, f32[2048,128]{1,0:T(8,128)S(1)}) custom-call(s32[1]{0:T(128)} %bitcast.1.refs_0_, f32[64,8,128]{2,1,0:T(8,128)S(1)} %get-tuple-element.34.refs_1_, f32[64,8,128]{2,1,0:T(8,128)S(1)} %get-tuple-element.33.refs_2_, f32[8,128]{1,0:T(8,128)S(1)} %copy-done.1, bf16[256,256]{1,0:T(8,128)(2,1)S(1)} %fusion.3.refs_4_, ...), custom_call_target="tpu_custom_call" | custom-call | flops 20000000000 | bytes 8388608 | tf_op jit(solution)/shard_map/grid_rows/pallas_call | solution.py:200
  49.8 8.1 %all-to-all-start.1 = ((f32[16,32,8,128]{3,2,1,0:T(8,128)}), f32[16,32,8,128]{3,2,1,0:T(8,128)}, u32[]{:S(2)}, u32[]{:S(2)}) async-start(f32[16,32,8,128]{3,2,1,0:T(8,128)} %get-tuple-element.14), calls=%async_computation.1 | async-start | bytes 4194304 | tf_op jit(solution)/shard_map/all_to_all | solution.py:405
  57.9 3.5 %collective-permute-start.1 = (f32[3,64,8,128]{3,2,1,0:T(8,128)S(1)}, f32[3,64,8,128]{3,2,1,0:T(8,128)S(1)}, u32[]{:S(2)}, u32[]{:S(2)}) collective-permute-start(f32[3,64,8,128]{3,2,1,0:T(8,128)S(1)} %copy-done.3), channel_id=1, source_target_pairs={{0,28},{1,29},{2,30},{3,31},{4,24},{5,25},{6,26},{7,27},{8,20},{9,... | collective-permute-start | bytes 2359304 | tf_op jit(solution)/shard_map/ppermute | solution.py:381
  61.4 40.1 %collective-permute-done.1 = f32[3,64,8,128]{3,2,1,0:T(8,128)S(1)} collective-permute-done((f32[3,64,8,128]{3,2,1,0:T(8,128)S(1)}, f32[3,64,8,128]{3,2,1,0:T(8,128)S(1)}, u32[]{:S(2)}, u32[]{:S(2)}) %collective-permute-start.1) | collective-permute-done | bytes 786464 | tf_op jit(solution)/shard_map/ppermute | solution.py:381
  101.6 0.1 bitcast_select_fusion.2
  101.7 13.7 %grid_rows.5 = (f32[16,32,8,128]{3,2,1,0:T(8,128)}, f32[2048,128]{1,0:T(8,128)S(1)}) custom-call(s32[1]{0:T(128)} %bitcast.1.refs_0_, f32[64,8,128]{2,1,0:T(8,128)S(1)} %get-tuple-element.22.refs_1_, f32[64,8,128]{2,1,0:T(8,128)S(1)} %get-tuple-element.31.refs_2_, f32[8,128]{1,0:T(8,128)S(1)} %copy-done.1, bf16[256,256]{1,0:T(8,128)(2,1)S(1)} %fusion.3.refs_4_, ...), custom_call_target="tpu_custom_call" | custom-call | flops 20000000000 | bytes 8388608 | tf_op jit(solution)/shard_map/grid_rows/pallas_call | solution.py:200
  115.4 0.0 all-to-all-done.1.refs_0_
  115.4 5.2 %all-to-all-start.2 = ((f32[16,32,8,128]{3,2,1,0:T(8,128)}), f32[16,32,8,128]{3,2,1,0:T(8,128)}, u32[]{:S(2)}, u32[]{:S(2)}) async-start(f32[16,32,8,128]{3,2,1,0:T(8,128)} %get-tuple-element.17), calls=%async_computation.2 | async-start | bytes 4194304 | tf_op jit(solution)/shard_map/all_to_all | solution.py:405
  120.6 13.7 %grid_rows.6 = (f32[16,32,8,128]{3,2,1,0:T(8,128)}, f32[2048,128]{1,0:T(8,128)S(1)}) custom-call(s32[1]{0:T(128)} %bitcast.1.refs_0_, f32[64,8,128]{2,1,0:T(8,128)S(1)} %get-tuple-element.32.refs_1_, f32[64,8,128]{2,1,0:T(8,128)S(1)} %get-tuple-element.21.refs_2_, f32[8,128]{1,0:T(8,128)S(1)} %copy-done.1, bf16[256,256]{1,0:T(8,128)(2,1)S(1)} %fusion.3.refs_4_, ...), custom_call_target="tpu_custom_call" | custom-call | flops 20000000000 | bytes 8388608 | tf_op jit(solution)/shard_map/grid_rows/pallas_call | solution.py:200
  134.2 13.0 %all-to-all-done.2.refs_1_ = f32[16,32,8,128]{3,2,1,0:T(8,128)} async-done(((f32[16,32,8,128]{3,2,1,0:T(8,128)}), f32[16,32,8,128]{3,2,1,0:T(8,128)}, u32[]{:S(2)}, u32[]{:S(2)}) %all-to-all-start.2) | async-done | bytes 2097184 | tf_op jit(solution)/shard_map/all_to_all | solution.py:405
  147.2 5.3 %all-to-all-start.3 = ((f32[16,32,8,128]{3,2,1,0:T(8,128)}), f32[16,32,8,128]{3,2,1,0:T(8,128)}, u32[]{:S(2)}, u32[]{:S(2)}) async-start(f32[16,32,8,128]{3,2,1,0:T(8,128)} %get-tuple-element.19), calls=%async_computation.3 | async-start | bytes 4194304 | tf_op jit(solution)/shard_map/all_to_all | solution.py:405
  152.5 16.3 %grid_rows.7 = f32[16,40,8,128]{3,2,1,0:T(8,128)} custom-call(s32[1]{0:T(128)} %bitcast.1.refs_0_, f32[64,8,128]{2,1,0:T(8,128)S(1)} %get-tuple-element.30.refs_1_, f32[64,8,128]{2,1,0:T(8,128)S(1)} %get-tuple-element.29.refs_2_, f32[8,128]{1,0:T(8,128)S(1)} %copy-done.1, bf16[256,256]{1,0:T(8,128)(2,1)S(1)} %fusion.3.refs_4_, ...), custom_call_target="tpu_custom_call" | custom-call | flops 20000000000 | bytes 8388608 | tf_op jit(solution)/shard_map/grid_rows/pallas_call | solution.py:200
  168.8 10.5 %all-to-all-done.3.refs_2_ = f32[16,32,8,128]{3,2,1,0:T(8,128)} async-done(((f32[16,32,8,128]{3,2,1,0:T(8,128)}), f32[16,32,8,128]{3,2,1,0:T(8,128)}, u32[]{:S(2)}, u32[]{:S(2)}) %all-to-all-start.3) | async-done | bytes 2097184 | tf_op jit(solution)/shard_map/all_to_all | solution.py:405
  179.4 4.2 %all-to-all-start.4 = ((f32[16,40,8,128]{3,2,1,0:T(8,128)}), f32[16,40,8,128]{3,2,1,0:T(8,128)S(1)}, u32[]{:S(2)}, u32[]{:S(2)}) async-start(f32[16,40,8,128]{3,2,1,0:T(8,128)} %grid_rows.7), calls=%async_computation.4 | async-start | bytes 5242880 | tf_op jit(solution)/shard_map/all_to_all | solution.py:405
  183.6 0.1 add.173
  183.7 0.2 negate_select_fusion.10
  183.9 0.1 reduce-precision_convert_fusion.3
  184.0 0.6 fusion.6.refs_7_
  184.6 0.2 fusion.49
  184.9 0.1 pad_maximum_fusion.2
  185.0 0.6 fusion.2
  185.6 0.7 pad_maximum_fusion.3.refs_4_
  186.3 29.7 %all-to-all-done.4.refs_3_ = f32[16,40,8,128]{3,2,1,0:T(8,128)S(1)} async-done(((f32[16,40,8,128]{3,2,1,0:T(8,128)}), f32[16,40,8,128]{3,2,1,0:T(8,128)S(1)}, u32[]{:S(2)}, u32[]{:S(2)}) %all-to-all-start.4) | async-done | bytes 2621472 | tf_op jit(solution)/shard_map/all_to_all | solution.py:405
  216.0 1.5 copy-done.2
  217.5 19.0 %columns.1 = f32[256,8192]{1,0:T(8,128)} custom-call(s32[1]{0:T(128)} %bitcast.flags_ref, f32[16,32,8,128]{3,2,1,0:T(8,128)} %all-to-all-done.1.refs_0_, f32[16,32,8,128]{3,2,1,0:T(8,128)} %all-to-all-done.2.refs_1_, f32[16,32,8,128]{3,2,1,0:T(8,128)} %all-to-all-done.3.refs_2_, f32[16,40,8,128]{3,2,1,0:T(8,128)} %copy-done.2, ...), custom_call_target="tpu_custom_call" | custom-call | tf_op jit(solution)/shard_map/columns/pallas_call | solution.py:322
  (20 shorter events, 0.2 us)
Async XLA Ops:
  5.1 18.8 %all-to-all-start = ((f32[4,4,16,8,128]{4,3,2,1,0:T(8,128)}), f32[4,4,16,8,128]{4,3,2,1,0:T(8,128)S(1)}, u32[]{:S(2)}, u32[]{:S(2)}) async-start(f32[4,4,16,8,128]{4,3,2,1,0:T(8,128)} %reverse_select_fusion.1), calls=%async_computation | async-start | bytes 2097152 | tf_op jit(solution)/shard_map/all_to_all | solution.py:374
  24.8 10.4 %collective-permute-start = (f32[1,64,8,128]{3,2,1,0:T(8,128)}, f32[1,64,8,128]{3,2,1,0:T(8,128)}, u32[]{:S(2)}, u32[]{:S(2)}) collective-permute-start(f32[1,64,8,128]{3,2,1,0:T(8,128)} %slice.46), channel_id=1, source_target_pairs={{0,28},{1,29},{2,30},{3,31},{4,24},{5,25},{6,26},{7,27},{8,20},{9,... | collective-permute-start | bytes 786440 | tf_op jit(solution)/shard_map/ppermute | solution.py:378
  27.1 125.4 %copy-start = (f32[2,64,128]{2,1,0:T(8,128)}, f32[2,64,128]{2,1,0:T(8,128)S(1)}, u32[]{:S(2)}) copy-start(f32[2,64,128]{2,1,0:T(8,128)S(1)} %pad_maximum_fusion.4.refs_5_.refs_6_) | copy-start | bytes 196612
  28.0 8.1 %copy-start.1 = (f32[8,128]{1,0:T(8,128)S(1)}, f32[8,128]{1,0:T(8,128)}, u32[]{:S(2)}) copy-start(f32[8,128]{1,0:T(8,128)} %refs_3_.7) | copy-start | bytes 12292
  49.8 8.1 %copy-start.3 = (f32[3,64,8,128]{3,2,1,0:T(8,128)S(1)}, f32[3,64,8,128]{3,2,1,0:T(8,128)}, u32[]{:S(2)}) copy-start(f32[3,64,8,128]{3,2,1,0:T(8,128)} %slice.45) | copy-start | bytes 2359300
  49.8 65.6 %all-to-all-start.1 = ((f32[16,32,8,128]{3,2,1,0:T(8,128)}), f32[16,32,8,128]{3,2,1,0:T(8,128)}, u32[]{:S(2)}, u32[]{:S(2)}) async-start(f32[16,32,8,128]{3,2,1,0:T(8,128)} %get-tuple-element.14), calls=%async_computation.1 | async-start | bytes 4194304 | tf_op jit(solution)/shard_map/all_to_all | solution.py:405
  57.9 43.7 %collective-permute-start.1 = (f32[3,64,8,128]{3,2,1,0:T(8,128)S(1)}, f32[3,64,8,128]{3,2,1,0:T(8,128)S(1)}, u32[]{:S(2)}, u32[]{:S(2)}) collective-permute-start(f32[3,64,8,128]{3,2,1,0:T(8,128)S(1)} %copy-done.3), channel_id=1, source_target_pairs={{0,28},{1,29},{2,30},{3,31},{4,24},{5,25},{6,26},{7,27},{8,20},{9,... | collective-permute-start | bytes 2359304 | tf_op jit(solution)/shard_map/ppermute | solution.py:381
  115.4 31.8 %all-to-all-start.2 = ((f32[16,32,8,128]{3,2,1,0:T(8,128)}), f32[16,32,8,128]{3,2,1,0:T(8,128)}, u32[]{:S(2)}, u32[]{:S(2)}) async-start(f32[16,32,8,128]{3,2,1,0:T(8,128)} %get-tuple-element.17), calls=%async_computation.2 | async-start | bytes 4194304 | tf_op jit(solution)/shard_map/all_to_all | solution.py:405
  147.2 32.1 %all-to-all-start.3 = ((f32[16,32,8,128]{3,2,1,0:T(8,128)}), f32[16,32,8,128]{3,2,1,0:T(8,128)}, u32[]{:S(2)}, u32[]{:S(2)}) async-start(f32[16,32,8,128]{3,2,1,0:T(8,128)} %get-tuple-element.19), calls=%async_computation.3 | async-start | bytes 4194304 | tf_op jit(solution)/shard_map/all_to_all | solution.py:405
  179.4 36.7 %all-to-all-start.4 = ((f32[16,40,8,128]{3,2,1,0:T(8,128)}), f32[16,40,8,128]{3,2,1,0:T(8,128)S(1)}, u32[]{:S(2)}, u32[]{:S(2)}) async-start(f32[16,40,8,128]{3,2,1,0:T(8,128)} %grid_rows.7), calls=%async_computation.4 | async-start | bytes 5242880 | tf_op jit(solution)/shard_map/all_to_all | solution.py:405
  216.0 1.5 copy-start.2
